TPU v7x, 256 devices: a whole 4x4x8 slice. The times are simulated.
256 devices in a mesh: section: 2 (over y_lo), expert: 8 (over y_hi, x), tensor: 16 (over z, core).
Axes of the slice: x: 4, y: 4 (y_hi: 2, y_lo: 2; y = y_hi * 2 + y_lo), z: 8, core: 2. Of those that a mesh axis runs over, the one named last changes fastest.
Arguments:
- query: bfloat16 [8, 1024, 4096], P('expert', 'tensor', 'section'), may hold values from -24 to 24
- keys: bfloat16 [8, 1024, 1024], P('expert', 'tensor', 'section'), may hold values from -24 to 24
- values: bfloat16 [8, 1024, 1024], P('expert', 'tensor', 'section'), may hold values from -6 to 6
- residual: bfloat16 [8, 1024, 4096], P('expert', 'tensor', 'section'), may hold values from -6 to 6
- routes: int32 [8, 1024, 2], P('expert', 'tensor'), may hold values from 0 to 7, all different within a row; in each aligned block of 64 rows (0 to 63, 64 to 127, ..., all dimensions but the last counted through in order) at most 17 rows name the same one
- gates: float32 [8, 1024, 2], P('expert', 'tensor'), may hold values from 0.1 to 0.9
- w_gate: bfloat16 [8, 4096, 8192], P('expert', None, 'tensor'), may hold values from -0.09375 to 0.09375
- w_up: bfloat16 [8, 4096, 8192], P('expert', None, 'tensor'), may hold values from -0.09375 to 0.09375
- w_down: bfloat16 [8, 8192, 4096], P('expert', 'tensor'), may hold values from -0.0625 to 0.0625
Outputs:
- layer_out: bfloat16 [8, 1024, 4096], P('expert', 'tensor', 'section')
Inputs may be any that keep to these rules, and one draw needn't show every extreme that they name: `routes`: the 2 entries of a row differ. In the rows of one index of expert and tensor (aligned blocks of 64 positions, taken in order over sequences and positions) no expert is named more than 17 times.
All inputs are finite; a program needn't handle non-finite values.
Results may differ from a plain program's by a relative error of at most 0.014.
Values may be sent and summed in bfloat16 or wider, within the bound.
A program may use at most 128 MiB of HBM per device.

v0:
```python
import math

import jax
import jax.numpy as jnp
from jax import lax
from jax.sharding import PartitionSpec as P

HD = 128
EXPERTS = 8
TOP = 2
HALF_CAP = 9


def in_one_piece(arrays, axis, dim, along):
    both = jnp.concatenate(arrays, axis=along)
    out, at, outs = (lax.all_gather(both, axis, axis=dim, tiled=True), 0, [])
    for a in arrays:
        outs.append(lax.slice_in_dim(out, at, at + a.shape[along], axis=along))
        at += a.shape[along]
    return tuple(outs)


def copy_for_each(shard, axis):
    devices = lax.axis_size(axis)
    return lax.all_to_all(
        jnp.broadcast_to(shard[None], (devices, *shard.shape)), axis, 0, 0, tiled=True
    )


def laid_out(tiles, dim):
    tiles = jnp.moveaxis(tiles, 0, dim)
    shape = tiles.shape
    return tiles.reshape(*shape[:dim], shape[dim] * shape[dim + 1], *shape[dim + 2 :])


def collect(shard, axis, dim):
    tiles = copy_for_each(shard, axis)
    return laid_out(tiles, dim)


def from_partner(value, axis, stride):
    mask = 2**stride
    pairs = [(source, source ^ mask) for source in range(lax.axis_size(axis))]
    return lax.ppermute(value, axis, pairs)


def slot_table(picked, first_slot, slot_count):
    flattened = picked.reshape(-1)
    onehot = (flattened[:, None] == jnp.arange(EXPERTS)[None, :]).astype(jnp.int32)
    before = jnp.cumsum(onehot, axis=0) - onehot
    slot_index = jnp.sum(before * onehot, axis=1)
    target = slot_index * EXPERTS + flattened
    rows_wanted = first_slot * EXPERTS + jnp.arange(slot_count * EXPERTS)
    return rows_wanted[:, None] == target[None, :]


def pack_rows(token_rows, picked, first_slot, slot_count):
    slot_hits = slot_table(picked, first_slot, slot_count)
    token_count = token_rows.shape[0]
    single = jnp.any(slot_hits.reshape(slot_count * EXPERTS, token_count, TOP), axis=2).astype(
        jnp.bfloat16
    )
    packed = jnp.dot(single, token_rows, preferred_element_type=jnp.float32).astype(jnp.bfloat16)
    return packed.reshape(slot_count, EXPERTS, token_rows.shape[1])


def expert_inner(piece_rows, gate_cols, up_cols):
    gate_part = jnp.einsum(
        "red,edf->ref", piece_rows, gate_cols, preferred_element_type=jnp.float32
    )
    up_part = jnp.einsum("red,edf->ref", piece_rows, up_cols, preferred_element_type=jnp.float32)
    return (jax.nn.silu(gate_part) * up_part).astype(jnp.bfloat16)


def on_device(query, keys, values, residual, routes, gates, w_gate, w_up, w_down):
    key_all, value_all = in_one_piece((keys, values), "tensor", 1, 0)
    token_count = query.shape[1]
    length = key_all.shape[1]
    half_width = query.shape[2]
    local_heads = half_width // HD
    local_kv = keys.shape[2] // HD
    groups = local_heads // local_kv
    section_id = lax.axis_index("section")
    queries = query[0].reshape(token_count, local_kv, groups, HD)
    key_heads = key_all[0].reshape(length, local_kv, HD)
    value_heads = value_all[0].reshape(length, local_kv, HD)
    scores = jnp.einsum(
        "qkgd,tkd->kgqt", queries, key_heads, preferred_element_type=jnp.float32
    ) / math.sqrt(HD)
    start_row = lax.axis_index("tensor") * token_count
    query_positions = start_row + jnp.arange(token_count)
    causal = query_positions[:, None] >= jnp.arange(length)[None, :]
    masked = jnp.where(causal, scores, -1e30)
    row_peak = jnp.max(masked, axis=-1, keepdims=True)
    exp_terms = jnp.where(causal, jnp.exp(masked - row_peak), 0.0)
    weights = (exp_terms / jnp.sum(exp_terms, axis=-1, keepdims=True)).astype(jnp.bfloat16)
    context = jnp.einsum("kgqt,tkd->qkgd", weights, value_heads, preferred_element_type=jnp.float32)
    hidden_half = (
        residual[0].astype(jnp.float32) + context.reshape(token_count, half_width)
    ).astype(jnp.bfloat16)
    picked = routes[0]
    hidden = collect(hidden_half, "section", 1)
    packed = pack_rows(hidden, picked, section_id * HALF_CAP, HALF_CAP)
    arrived = lax.all_to_all(packed, "expert", split_axis=1, concat_axis=0, tiled=True)
    inner_rows = expert_inner(lax.all_gather(arrived, "tensor", axis=0, tiled=True), w_gate, w_up)
    summed = lax.psum_scatter(
        jnp.einsum("ref,efd->red", inner_rows, w_down, preferred_element_type=jnp.float32).astype(
            jnp.bfloat16
        ),
        "tensor",
        scatter_dimension=0,
        tiled=True,
    )
    returned = lax.all_to_all(summed, "expert", split_axis=0, concat_axis=1, tiled=True)
    own_cols = lax.dynamic_slice_in_dim(returned, section_id * half_width, half_width, 2)
    other_cols = lax.dynamic_slice_in_dim(returned, (1 - section_id) * half_width, half_width, 2)
    partner_cols = from_partner(other_cols, "section", 0)
    first_half = jnp.where(section_id == 0, own_cols, partner_cols)
    second_half = jnp.where(section_id == 0, partner_cols, own_cols)
    returned_half = jnp.concatenate([first_half, second_half], axis=0)
    slot_total = returned_half.shape[0]
    slot_hits = slot_table(picked, 0, slot_total)
    weight_table = jnp.sum(
        slot_hits.astype(jnp.float32).reshape(slot_total * EXPERTS, token_count, TOP)
        * gates[0][None, :, :],
        axis=2,
    )
    expert_sum = jnp.einsum(
        "ct,cd->td",
        weight_table,
        returned_half.reshape(slot_total * EXPERTS, half_width).astype(jnp.float32),
    )
    layer_out = (hidden_half.astype(jnp.float32) + expert_sum).astype(jnp.bfloat16)
    return layer_out[None]


def solution(mesh):
    return jax.shard_map(
        on_device,
        mesh=mesh,
        in_specs=(
            P("expert", "tensor", "section"),
            P("expert", "tensor", "section"),
            P("expert", "tensor", "section"),
            P("expert", "tensor", "section"),
            P("expert", "tensor", None),
            P("expert", "tensor", None),
            P("expert", None, "tensor"),
            P("expert", None, "tensor"),
            P("expert", "tensor", None),
        ),
        out_specs=P("expert", "tensor", "section"),
        check_vma=False,
    )
```

profile of v0, /device:TPU:96, one launch (start us, length us, event | category | flops | bytes accessed | tf_op | source)
XLA Modules:
  0.0 314.1 jit_solution(3981826981273783136)
XLA Ops:
  6.5 0.9 copy.59
  7.5 0.9 copy.60
  8.4 1.0 pad_maximum_fusion.1
  9.4 1.1 reshape_squeeze.15
  10.5 0.8 copy.67
  12.2 37.9 %all-gather.3.cloned.1.call-done = bf16[2,1024,512]{2,0,1:T(2,128)(2,1)} async-done(((bf16[2,64,512]{2,0,1:T(2,128)(2,1)}), bf16[2,1024,512]{2,0,1:T(2,128)(2,1)}) %all-gather.3.cloned.1.call-update) | async-done | bytes 2097168 | tf_op jit(solution)/shard_map/all_gather | solution.py:16
  50.2 6.4 %fusion.72 = (bf16[1,1024,512]{2,0,1:T(2,128)(2,1)}, bf16[1,1024,512]{2,0,1:T(2,128)(2,1)S(1)}) fusion(bf16[2,1024,512]{2,0,1:T(2,128)(2,1)} %all-gather.3.cloned.1.call-done), kind=kLoop, calls=%fused_computation.66 | loop fusion | bytes 4194304 | tf_op jit(solution)/shard_map/slice | solution.py:18
  56.6 4.6 %copy.82 = bf16[1,1024,512]{1,2,0:T(8,128)(2,1)S(1)} copy(bf16[1,1024,512]{2,0,1:T(2,128)(2,1)} %get-tuple-element.5) | data formatting | bytes 2097152
  61.2 4.3 %copy.81 = bf16[1,1024,512]{1,2,0:T(8,128)(2,1)} copy(bf16[1,1024,512]{2,0,1:T(2,128)(2,1)S(1)} %get-tuple-element.6) | data formatting | bytes 2097152
  65.4 3.7 %fusion.73 = (f32[4,4,64]{2,1,0:T(4,128)S(1)}, f32[4,4,64,1024]{3,2,1,0:T(8,128)}) fusion(pred[64,1024]{1,0:T(8,128)(4,1)S(1)} %iota_compare_fusion, bf16[1024,4,128,1]{0,2,3,1:T(8,128)(2,1)S(1)} %bitcast.137, bf16[64,4,4,128]{3,2,1,0:T(4,128)(2,1)S(1)} %reshape_squeeze.15), kind=kOutput, calls=%fused_computation.67 | convolution fusion | flops 273679360 | bytes 5574656 | tf_op jit(solution)/shard_map/sub | solution.py:95
  69.1 3.0 fusion.51
  72.7 0.8 broadcast_in_dim.37
  73.6 3.5 %all-to-all-start = ((bf16[2,64,2048]{2,1,0:T(8,128)(2,1)}), bf16[2,64,2048]{2,1,0:T(8,128)(2,1)S(1)}, u32[]{:S(2)}, u32[]{:S(2)}) async-start(bf16[2,64,2048]{2,1,0:T(8,128)(2,1)} %broadcast_in_dim.37), calls=%async_computation | async-start | bytes 1048576 | tf_op jit(solution)/shard_map/all_to_all | solution.py:25
  77.3 8.4 %all-to-all-done = bf16[2,64,2048]{2,1,0:T(8,128)(2,1)S(1)} async-done(((bf16[2,64,2048]{2,1,0:T(8,128)(2,1)}), bf16[2,64,2048]{2,1,0:T(8,128)(2,1)S(1)}, u32[]{:S(2)}, u32[]{:S(2)}) %all-to-all-start) | async-done | bytes 524320 | tf_op jit(solution)/shard_map/all_to_all | solution.py:25
  86.1 0.4 copy.71
  86.5 23.2 %all_to_all.35 = bf16[9,8,4096]{2,0,1:T(8,128)(2,1)S(1)} all-to-all(bf16[9,8,4096]{2,0,1:T(8,128)(2,1)S(1)} %copy.71), channel_id=1, replica_groups=mesh['section'=2,'expert'=8,'tensor'=16] {'expert'}, dimensions={1} | all-to-all | bytes 1179648 | tf_op jit(solution)/shard_map/all_to_all | solution.py:104
  109.7 1.1 all_to_all.29
  111.0 55.2 %all-gather.5.cloned.1.call-done = bf16[1152,1,4096]{2,0,1:T(8,128)(2,1)} async-done(((bf16[72,1,4096]{2,0,1:T(8,128)(2,1)}), bf16[1152,1,4096]{2,0,1:T(8,128)(2,1)}) %all-gather.5.cloned.1.call-update) | async-done | bytes 9437200 | tf_op jit(solution)/shard_map/all_gather | solution.py:105
  166.2 9.9 %fusion.10 = f32[1152,1,512]{2,0,1:T(8,128)} fusion(bf16[1,4096,512]{2,1,0:T(8,128)(2,1)} %param.15, bf16[1152,1,4096]{2,0,1:T(8,128)(2,1)} %all-gather.5.cloned.1.call-done), kind=kOutput, calls=%fused_computation.15 | convolution fusion | flops 4831838208 | bytes 15990784 | tf_op jit(solution)/shard_map/red,edf->ref/dot_general | solution.py:68
  176.1 17.6 %fusion.1 = bf16[1152,1,4096]{2,0,1:T(8,128)(2,1)} fusion(bf16[1,512,4096]{2,1,0:T(8,128)(2,1)} %param.17, bf16[1,4096,512]{2,1,0:T(8,128)(2,1)} %param.16, bf16[1152,1,4096]{2,0,1:T(8,128)(2,1)} %all-gather.5.cloned.1.call-done, f32[1152,1,512]{2,0,1:T(8,128)} %fusion.10), kind=kOutput, calls=%fused_computation.2 | convolution fusion | flops 9671933952 | bytes 29622272 | tf_op jit(solution)/shard_map/ref,efd->red/dot_general | solution.py:107
  193.7 68.5 %reduce-scatter.2.cloned.1.call-done = bf16[72,1,4096]{2,0,1:T(8,128)(2,1)} async-done(((bf16[1152,1,4096]{2,0,1:T(8,128)(2,1)}), bf16[72,1,4096]{2,0,1:T(8,128)(2,1)}) %reduce-scatter.2.cloned.1.call-update) | async-done | bytes 589840 | tf_op jit(solution)/shard_map/reduce_scatter | solution.py:106
  262.2 0.5 broadcast.48
  262.7 2.1 reduce.1
  264.8 1.4 reshape.95
  266.2 6.7 %all-to-all-start.2 = ((bf16[8,2,18432]{2,1,0:T(2,128)(2,1)}), bf16[8,2,18432]{2,1,0:T(2,128)(2,1)S(1)}, u32[]{:S(2)}, u32[]{:S(2)}) async-start(bf16[8,2,18432]{2,1,0:T(2,128)(2,1)} %reshape.95), calls=%async_computation.3 | async-start | bytes 1179648 | tf_op jit(solution)/shard_map/all_to_all | solution.py:114
  272.9 13.2 %all-to-all-done.2 = bf16[8,2,18432]{2,1,0:T(2,128)(2,1)S(1)} async-done(((bf16[8,2,18432]{2,1,0:T(2,128)(2,1)}), bf16[8,2,18432]{2,1,0:T(2,128)(2,1)S(1)}, u32[]{:S(2)}, u32[]{:S(2)}) %all-to-all-start.2) | async-done | bytes 589856 | tf_op jit(solution)/shard_map/all_to_all | solution.py:114
  286.1 0.6 reshape.96
  286.6 3.6 %reduce = bf16[72,4096]{1,0:T(8,128)(2,1)S(1)} reduce(bf16[72,1,4096]{2,1,0:T(2,128)(2,1)S(1)} %reshape.96, bf16[]{:T(256)} %constant.57), dimensions={1}, to_apply=%all_to_all.30.reduce_sub_computation | reduce | bytes 1179650 | tf_op jit(solution)/shard_map/all_to_all | solution.py:114
  290.5 0.6 collective-permute-start
  291.5 13.4 %collective-permute-done = bf16[9,8,2048]{2,0,1:T(8,128)(2,1)} collective-permute-done((bf16[9,8,2048]{2,0,1:T(8,128)(2,1)S(1)}, bf16[9,8,2048]{2,0,1:T(8,128)(2,1)}, u32[]{:S(2)}, u32[]{:S(2)}) %collective-permute-start) | collective-permute-done | bytes 294944 | tf_op jit(solution)/shard_map/ppermute | solution.py:44
  304.9 1.3 bitcast_select_fusion.5
  306.4 1.2 fusion.46
  (36 shorter events, 3.1 us)
Async XLA Ops:
  6.5 43.6 %all-gather.3.cloned.1.call-start = ((), (), s32[]{:S(2)}) async-start(), calls=%async_computation.4 | async-start | bytes 2228224 | tf_op jit(solution)/shard_map/all_gather | solution.py:16
  65.4 3.7 %copy-start = (bf16[1,1024,512]{1,2,0:T(8,128)(2,1)S(1)}, bf16[1,1024,512]{1,2,0:T(8,128)(2,1)}, u32[]{:S(2)}) copy-start(bf16[1,1024,512]{1,2,0:T(8,128)(2,1)} %copy.81) | copy-start | bytes 3145732
  69.1 3.6 %copy-start.1 = (bf16[1,64,2048]{2,1,0:T(8,128)(2,1)S(1)}, bf16[1,64,2048]{2,1,0:T(8,128)(2,1)}, u32[]{:S(2)}) copy-start(bf16[1,64,2048]{2,1,0:T(8,128)(2,1)} %param.12) | copy-start | bytes 786436
  72.1 5.0 %copy-start.2 = (s32[1,64,2]{1,2,0:T(2,128)S(1)}, s32[1,64,2]{1,2,0:T(2,128)}, u32[]{:S(2)}) copy-start(s32[1,64,2]{1,2,0:T(2,128)} %param.13) | copy-start | bytes 1540
  73.6 12.1 %all-to-all-start = ((bf16[2,64,2048]{2,1,0:T(8,128)(2,1)}), bf16[2,64,2048]{2,1,0:T(8,128)(2,1)S(1)}, u32[]{:S(2)}, u32[]{:S(2)}) async-start(bf16[2,64,2048]{2,1,0:T(8,128)(2,1)} %broadcast_in_dim.37), calls=%async_computation | async-start | bytes 1048576 | tf_op jit(solution)/shard_map/all_to_all | solution.py:25
  77.1 89.2 %all-gather.5.cloned.1.call-start = ((), (), s32[]{:S(2)}) async-start(), calls=%async_computation.5 | async-start | bytes 10027008 | tf_op jit(solution)/shard_map/all_gather | solution.py:105
  110.8 151.4 %reduce-scatter.2.cloned.1.call-start = ((), (), s32[]{:S(2)}) async-start(), calls=%async_computation.6 | async-start | bytes 10027008 | tf_op jit(solution)/shard_map/reduce_scatter | solution.py:106
  264.8 26.3 %copy-start.3 = (f32[1,64,2]{1,2,0:T(2,128)S(1)}, f32[1,64,2]{1,2,0:T(2,128)}, u32[]{:S(2)}) copy-start(f32[1,64,2]{1,2,0:T(2,128)} %param.14) | copy-start | bytes 1540
  266.2 19.9 %all-to-all-start.2 = ((bf16[8,2,18432]{2,1,0:T(2,128)(2,1)}), bf16[8,2,18432]{2,1,0:T(2,128)(2,1)S(1)}, u32[]{:S(2)}, u32[]{:S(2)}) async-start(bf16[8,2,18432]{2,1,0:T(2,128)(2,1)} %reshape.95), calls=%async_computation.3 | async-start | bytes 1179648 | tf_op jit(solution)/shard_map/all_to_all | solution.py:114
  290.5 14.4 %collective-permute-start = (bf16[9,8,2048]{2,0,1:T(8,128)(2,1)S(1)}, bf16[9,8,2048]{2,0,1:T(8,128)(2,1)}, u32[]{:S(2)}, u32[]{:S(2)}) collective-permute-start(bf16[9,8,2048]{2,0,1:T(8,128)(2,1)S(1)} %dynamic-slice_bitcast_fusion), channel_id=1, source_target_pairs={{0,128},{128,0},{1,129},{129,1},{2,130},{130,2},{3,131},{131,3},{4... | collective-permute-start | bytes 884744 | tf_op jit(solution)/shard_map/ppermute | solution.py:44
Sparse Core Ops, SparseCore 0:
  9.5 40.5 all-gather.2
  110.9 55.2 all-gather.4
  193.9 68.3 reduce-scatter.1
where the time goes:
time: 315 us; the launch traced here: 314 us
  waiting for transfers between devices  197 us (63%)
  matrix products  35.6 us (11%)
  local copies, waits for them, and re-layouts  25.2 us (8%)
  blocking collectives  23.2 us (7%)
  between operations  13.4 us (4%)
  starting transfers between devices  11.1 us (4%)
  other arithmetic  8.89 us (3%)
    reduce_scatter x1, waiting for transfers between devices, on_device(): lax.psum_scatter(jnp.einsum('ref,efd->red', inner_rows, w_down, preferred...  68.5 us
    all_gather x1, waiting for transfers between devices, on_device(): lax.all_gather(arrived, 'tensor', axis=0, tiled=True)  55.2 us
    all_gather x1, waiting for transfers between devices, in_one_piece(): out, at, outs = (lax.all_gather(both, axis, axis=dim, tiled=True), 0, [])  37.9 us
    all_to_all x1, blocking collectives, on_device(): lax.all_to_all(packed, 'expert', split_axis=1, concat_axis=0, tiled=True)  23.2 us
    dot_general x1, matrix products, on_device(): jnp.einsum('ref,efd->red', inner_rows, w_down, preferred_element_type=jnp...  17.6 us
    unnamed x15, local copies, waits for them, and re-layouts  13.4 us
    ppermute x1, waiting for transfers between devices, from_partner(): return lax.ppermute(value, axis, pairs)  13.4 us
    all_to_all x1, waiting for transfers between devices, on_device(): lax.all_to_all(summed, 'expert', split_axis=0, concat_axis=1, tiled=True)  13.2 us
  transfers between devices with their start and end apart: 6, of which 6 were waited for; matrix products, arithmetic and copies ran while one was open for 1% of the time, Pallas kernels for 0%

commit v1 on v0

v1 whole, which is shorter than its diff:
```python
import math

import jax
import jax.numpy as jnp
from jax import lax
from jax.experimental import pallas as pl
from jax.experimental.pallas import tpu as pltpu
from jax.sharding import PartitionSpec as P

HD = 128
EXPERTS = 8
NZ = 8
SLOTS = 8
MAIN = 2 * SLOTS * EXPERTS
ROWS = MAIN + EXPERTS
CHUNKS = 4
MESH = pl.DeviceIdType.MESH
BF = jnp.bfloat16
F32 = jnp.float32


def dot(a, b):
    return jnp.dot(a, b, preferred_element_type=F32)


def copy_to(src, dst, send, recv, device):
    return pltpu.make_async_remote_copy(
        src_ref=src, dst_ref=dst, send_sem=send, recv_sem=recv, device_id=device, device_id_type=MESH
    )


def moe_kernel(
    hid, pm, po, gm, go, wg_any, wu_any, wd_any, out,
    wg, wu, wd, pk, pov, xr, ovr, xm, xp, inner, yps, ypr, ys, rr, fr, fov, ret, retov,
    w_sem, d_s, d_r, o_s, o_r, ag_s, ag_r, xs, xrs, yss, yrs, rs_s, rs_r, b_s, b_r, bo_s, bo_r,
):
    s, e, t = lax.axis_index("section"), lax.axis_index("expert"), lax.axis_index("tensor")
    z, c = t // 2, t % 2
    half = hid.shape[1]
    cw = half // CHUNKS
    barrier = pltpu.get_barrier_semaphore()
    for i in range(1, 32):
        other = (s * 2 + c) ^ (i % 4)
        pl.semaphore_signal(
            barrier, inc=1, device_id=(other // 2, (e + i // 4) % 8, z * 2 + other % 2), device_id_type=MESH
        )
    up, down = (z + 1) % NZ, (z + NZ - 1) % NZ
    for near in (up, down):
        pl.semaphore_signal(barrier, inc=1, device_id=(s, e, near * 2 + c), device_id_type=MESH)
    loads = []
    for part in range(2):
        h = (c + part) % 2
        rows = pl.ds(pl.multiple_of(h * half, half), half)
        loads.append(pltpu.make_async_copy(wg_any.at[0, rows, :], wg.at[part], w_sem.at[part]))
        loads.append(pltpu.make_async_copy(wu_any.at[0, rows, :], wu.at[part], w_sem.at[2 + part]))
        loads.append(pltpu.make_async_copy(wd_any.at[0, :, rows], wd.at[part], w_sem.at[4 + part]))
    for load in loads:
        load.start()

    tokens = hid[...]
    pk[...] = dot(pm[...], tokens).astype(BF).reshape(pk.shape)
    extra = dot(po[...], tokens)
    for j in range(16):
        pov[:, j, :] = extra[:, 128 * j : 128 * (j + 1)]
    pl.semaphore_wait(barrier, 33)

    own = s == c
    sent = []
    for i in range(8):
        ed = (e + i) % 8
        main = []
        for k in range(2):
            sd = (s + k) % 2
            main.append(
                copy_to(pk.at[ed * 2 + sd], xr.at[e * 2 + c], d_s.at[i * 2 + k], d_r.at[e * 2 + c], (sd, ed, z * 2 + s))
            )
        over = copy_to(pov.at[ed], ovr.at[e], o_s.at[i], o_r.at[e], (c, ed, z * 2 + s))
        main[1].start()
        if i == 0:
            @pl.when(own)
            def _():
                xr[e * 2 + c] = pk[e * 2 + s]
                ovr[e] = pov[e]

            @pl.when(jnp.logical_not(own))
            def _():
                main[0].start()
                over.start()
            own_main, own_over = main[0], over
        else:
            main[0].start()
            over.start()
            sent += [main[0], over]
        sent.append(main[1])
    for i in range(8):
        ef = (e + 8 - i) % 8
        for k in range(2):
            cf = (c + k) % 2
            arrival = copy_to(pk.at[0], xr.at[ef * 2 + cf], d_s.at[0], d_r.at[ef * 2 + cf], (c, ef, z * 2 + cf))
            if i == 0 and k == 0:
                pl.when(jnp.logical_not(own))(arrival.wait_recv)
            else:
                arrival.wait_recv()
        arrival = copy_to(pov.at[0], ovr.at[ef], o_s.at[0], o_r.at[ef], (c, ef, z * 2 + s))
        if i == 0:
            pl.when(jnp.logical_not(own))(arrival.wait_recv)
        else:
            arrival.wait_recv()
    xm[7, :MAIN, :] = xr[...].reshape(MAIN, half)
    for j in range(16):
        xm[7, MAIN:, 128 * j : 128 * (j + 1)] = ovr[:, j, :].astype(BF)

    def slot(way, d):
        return 7 if d == 0 else 6 if d == 4 else 2 * (d - 1) + way

    def cols(j):
        return pl.ds(cw * j, cw)

    partner = (s, e, z * 2 + 1 - c)
    ring = ((s, e, up * 2 + c), (s, e, down * 2 + c))
    half_of = ((0, 1), (2, 3))
    gather, share = {}, {}
    for way in range(2):
        for d in range(4):
            for j in range(CHUNKS) if d < 3 else half_of[way]:
                n = d * 4 + j
                gather[way, d, j] = copy_to(
                    xm.at[slot(way, d), :, cols(j)], xm.at[slot(way, d + 1), :, cols(j)],
                    ag_s.at[way, n], ag_r.at[way, n], ring[way],
                )
    for k in range(8):
        share[k] = copy_to(xm.at[k], xp.at[k], xs.at[k], xrs.at[k], partner)
    trade = {
        g: copy_to(yps.at[pl.ds(2 * g - 2, 2)], ypr.at[pl.ds(2 * g - 2, 2)], yss.at[g - 1], yrs.at[g - 1], partner)
        for g in range(1, 5)
    }

    def hidden_units(g, first, last):
        def piece(k, carry):
            at = pl.ds(pl.multiple_of(k * 256, 256), 256)
            left = xm[2 * g - 2 : 2 * g].reshape(2 * ROWS, half)
            right = xp[2 * g - 2 : 2 * g].reshape(2 * ROWS, half)
            gate = dot(left, wg[0, :, at]) + dot(right, wg[1, :, at])
            lift = dot(left, wu[0, :, at]) + dot(right, wu[1, :, at])
            inner[pl.ds((2 * g - 2) * ROWS, 2 * ROWS), at] = (gate / (1.0 + jnp.exp(-gate)) * lift).astype(BF)
            return carry

        lax.fori_loop(first, last, piece, 0)

    def down_out(g):
        rows = inner[pl.ds((2 * g - 2) * ROWS, 2 * ROWS), :]

        def theirs(j, carry):
            at = pl.ds(pl.multiple_of(j * cw, cw), cw)
            yps[pl.ds(2 * g - 2, 2), :, at] = dot(rows, wd[1, :, at]).astype(BF).reshape(2, ROWS, cw)
            return carry

        lax.fori_loop(0, CHUNKS, theirs, 0)
        trade[g].start()

    def down_own(g):
        rows = inner[pl.ds((2 * g - 2) * ROWS, 2 * ROWS), :]
        trade[g].wait_recv()

        def mine(j, carry):
            at = pl.ds(pl.multiple_of(j * cw, cw), cw)
            both = dot(rows, wd[0, :, at]).reshape(2, ROWS, cw) + ypr[pl.ds(2 * g - 2, 2), :, at].astype(F32)
            ys[pl.ds(2 * g - 2, 2), :, at] = both.astype(BF)
            return carry

        lax.fori_loop(0, CHUNKS, mine, 0)

    for j in range(CHUNKS):
        gather[0, 0, j].start()
        gather[1, 0, j].start()
    share[7].start()
    for load in loads:
        load.wait()
    for d in range(1, 5):
        if d > 1:
            for way in range(2):
                share[slot(way, d - 1)].wait_recv()
        for j in range(CHUNKS):
            for way in range(2):
                if d < 4 or j in half_of[way]:
                    gather[way, d - 1, j].wait_recv()
                    if (way, d, j) in gather:
                        gather[way, d, j].start()
                if d < 4 and j == CHUNKS - 1:
                    share[slot(way, d)].start()
            if d in (2, 3) and j % 2 == 1:
                hidden_units(d - 1, j // 2, j // 2 + 1)
        if d == 4:
            share[6].start()
            hidden_units(3, 0, 2)
    down_out(3)
    down_own(3)

    reduce = {}
    for way in range(2):
        for d in range(1, 5):
            target = slot(1 - way, d)
            for j in range(CHUNKS) if d < 4 else half_of[way]:
                n = (d - 1) * 4 + j
                reduce[way, d, j] = copy_to(
                    ys.at[target, :, cols(j)], rr.at[way, d - 1, :, cols(j)],
                    rs_s.at[way, n], rs_r.at[way, n], ring[way],
                )

    def pass_on(way, d, j, add):
        if add:
            reduce[way, d + 1, j].wait_recv()
            k = slot(1 - way, d)
            total = ys[k, :, cols(j)].astype(F32) + rr[way, d, :, cols(j)].astype(F32)
            ys[k, :, cols(j)] = total.astype(BF)
        reduce[way, d, j].start()

    for n in range(2):
        for way in range(2):
            pass_on(way, 3, half_of[1 - way][n], False)
    share[6].wait_recv()
    share[7].wait_recv()
    hidden_units(4, 0, 2)
    down_out(4)
    down_own(4)
    for n in range(2):
        for way in range(2):
            pass_on(way, 4, half_of[way][n], False)
    down_out(2)
    for n in range(2):
        for way in range(2):
            pass_on(way, 3, half_of[way][n], True)
    down_own(2)
    down_out(1)
    for h in range(2):
        for n in range(2):
            for way in range(2):
                pass_on(way, 2, half_of[1 - way if h == 0 else way][n], True)
    down_own(1)
    for h in range(2):
        for n in range(2):
            for way in range(2):
                pass_on(way, 1, half_of[1 - way if h == 0 else way][n], True)

    for j in range(CHUNKS):
        for way in range(2):
            reduce[way, 1, j].wait_recv()
        total = (
            ys[7, :, cols(j)].astype(F32) + rr[0, 0, :, cols(j)].astype(F32) + rr[1, 0, :, cols(j)].astype(F32)
        ).astype(BF)
        fr[:, :, cols(j)] = total[:MAIN].reshape(2 * EXPERTS, SLOTS, cw)
        tail = total[MAIN:].astype(F32)
        for k in range(cw // 128):
            fov[:, j * (cw // 128) + k, :] = tail[:, 128 * k : 128 * (k + 1)]

    for i in range(8):
        ed = (e + i) % 8
        main = []
        for k in range(2):
            cd = (c + k) % 2
            main.append(
                copy_to(fr.at[ed * 2 + cd], ret.at[e * 2 + s], b_s.at[i * 2 + k], b_r.at[e * 2 + s], (c, ed, z * 2 + cd))
            )
        over = copy_to(fov.at[ed], retov.at[e], bo_s.at[i], bo_r.at[e], (c, ed, z * 2 + s))
        main[1].start()
        if i == 0:
            @pl.when(own)
            def _():
                ret[e * 2 + s] = fr[e * 2 + c]
                retov[e] = fov[e]

            @pl.when(jnp.logical_not(own))
            def _():
                main[0].start()
                over.start()
            back_main, back_over = main[0], over
        else:
            main[0].start()
            over.start()
            sent += [main[0], over]
        sent.append(main[1])
    for i in range(8):
        ef = (e + 8 - i) % 8
        for k in range(2):
            sf = (s + k) % 2
            arrival = copy_to(fr.at[0], ret.at[ef * 2 + sf], b_s.at[0], b_r.at[ef * 2 + sf], (sf, ef, z * 2 + s))
            if i == 0 and k == 0:
                pl.when(jnp.logical_not(own))(arrival.wait_recv)
            else:
                arrival.wait_recv()
        arrival = copy_to(fov.at[0], retov.at[ef], bo_s.at[0], bo_r.at[ef], (c, ef, z * 2 + s))
        if i == 0:
            pl.when(jnp.logical_not(own))(arrival.wait_recv)
        else:
            arrival.wait_recv()

    rows = ret[...].reshape(MAIN, half)
    total = hid[...].astype(F32)
    for weight, part in ((gm, rows), (go, jnp.concatenate([retov[:, j, :] for j in range(16)], axis=1).astype(BF))):
        high = weight[...].astype(BF)
        low = (weight[...] - high.astype(F32)).astype(BF)
        total = total + dot(high, part) + dot(low, part)
    out[...] = total.astype(BF)

    @pl.when(jnp.logical_not(own))
    def _():
        for copy in (own_main, own_over, back_main, back_over):
            copy.wait_send()
    for copy in sent:
        copy.wait_send()
    for table in (gather, share, trade, reduce):
        for copy in table.values():
            copy.wait_send()


def moe(hidden, pm, po, gm, go, w_gate, w_up, w_down):
    half = hidden.shape[1]
    units = w_gate.shape[2]
    vmem = pl.BlockSpec(memory_space=pltpu.VMEM)
    hbm = pl.BlockSpec(memory_space=pl.ANY)
    dma = pltpu.SemaphoreType.DMA
    return pl.pallas_call(
        moe_kernel,
        out_shape=jax.ShapeDtypeStruct(hidden.shape, BF),
        in_specs=[vmem] * 5 + [hbm] * 3,
        out_specs=vmem,
        scratch_shapes=[
            pltpu.VMEM((2, half, units), BF),
            pltpu.VMEM((2, half, units), BF),
            pltpu.VMEM((2, units, half), BF),
            pltpu.VMEM((16, SLOTS, half), BF),
            pltpu.VMEM((8, 16, 128), F32),
            pltpu.VMEM((16, SLOTS, half), BF),
            pltpu.VMEM((8, 16, 128), F32),
            pltpu.VMEM((8, ROWS, half), BF),
            pltpu.VMEM((8, ROWS, half), BF),
            pltpu.VMEM((8 * ROWS, units), BF),
            pltpu.VMEM((8, ROWS, half), BF),
            pltpu.VMEM((8, ROWS, half), BF),
            pltpu.VMEM((8, ROWS, half), BF),
            pltpu.VMEM((2, 4, ROWS, half), BF),
            pltpu.VMEM((16, SLOTS, half), BF),
            pltpu.VMEM((8, 16, 128), F32),
            pltpu.VMEM((16, SLOTS, half), BF),
            pltpu.VMEM((8, 16, 128), F32),
            dma((6,)), dma((16,)), dma((16,)), dma((8,)), dma((8,)),
            dma((2, 16)), dma((2, 16)), dma((8,)), dma((8,)), dma((4,)), dma((4,)),
            dma((2, 16)), dma((2, 16)), dma((16,)), dma((16,)), dma((8,)), dma((8,)),
        ],
        compiler_params=pltpu.CompilerParams(
            collective_id=1, has_side_effects=True, vmem_limit_bytes=60 * 1024 * 1024
        ),
        name="moe",
    )(hidden, pm, po, gm, go, w_gate, w_up, w_down)


def tables(picked, gates):
    hits = picked[:, :, None] == jnp.arange(EXPERTS)
    named = jnp.any(hits, axis=1)
    gate = jnp.sum(jnp.where(hits, gates[:, :, None], 0.0), axis=1)
    place = jnp.cumsum(named.astype(jnp.int32), axis=0) - named.astype(jnp.int32)
    tokens = picked.shape[0]
    main = named[:, :, None] & (place[:, :, None] == jnp.arange(2 * SLOTS))
    gm = jnp.where(main, gate[:, :, None], 0.0).reshape(tokens, MAIN)
    over = named & (place == 2 * SLOTS)
    go = jnp.where(over, gate, 0.0)
    return main.reshape(tokens, MAIN).T.astype(BF), over.T.astype(BF), gm, go


def on_device(query, keys, values, residual, routes, gates, w_gate, w_up, w_down):
    both = lax.all_gather(jnp.concatenate((keys, values), axis=0), "tensor", axis=1, tiled=True)
    key_all, value_all = both[0], both[1]
    token_count = query.shape[1]
    length = key_all.shape[0]
    half_width = query.shape[2]
    local_heads = half_width // HD
    local_kv = keys.shape[2] // HD
    groups = local_heads // local_kv
    queries = query[0].reshape(token_count, local_kv, groups, HD)
    key_heads = key_all.reshape(length, local_kv, HD)
    value_heads = value_all.reshape(length, local_kv, HD)
    scores = jnp.einsum(
        "qkgd,tkd->kgqt", queries, key_heads, preferred_element_type=F32
    ) / math.sqrt(HD)
    start_row = lax.axis_index("tensor") * token_count
    query_positions = start_row + jnp.arange(token_count)
    causal = query_positions[:, None] >= jnp.arange(length)[None, :]
    masked = jnp.where(causal, scores, -1e30)
    row_peak = jnp.max(masked, axis=-1, keepdims=True)
    exp_terms = jnp.where(causal, jnp.exp(masked - row_peak), 0.0)
    weights = (exp_terms / jnp.sum(exp_terms, axis=-1, keepdims=True)).astype(BF)
    context = jnp.einsum("kgqt,tkd->qkgd", weights, value_heads, preferred_element_type=F32)
    hidden = (residual[0].astype(F32) + context.reshape(token_count, half_width)).astype(BF)
    pm, po, gm, go = tables(routes[0], gates[0])
    return moe(hidden, pm, po, gm, go, w_gate, w_up, w_down)[None]


def solution(mesh):
    return jax.shard_map(
        on_device,
        mesh=mesh,
        in_specs=(
            P("expert", "tensor", "section"),
            P("expert", "tensor", "section"),
            P("expert", "tensor", "section"),
            P("expert", "tensor", "section"),
            P("expert", "tensor", None),
            P("expert", "tensor", None),
            P("expert", None, "tensor"),
            P("expert", None, "tensor"),
            P("expert", "tensor", None),
        ),
        out_specs=P("expert", "tensor", "section"),
        check_vma=False,
    )
```

time: 315 us -> 213 us (0.68)
  the two profiles are of different devices: /device:TPU:96 before, /device:TPU:1 now
where the time goes in v1:
time: 213 us
  Pallas kernels  127 us (60%)
  waiting for transfers between devices  37.8 us (18%)
  local copies, waits for them, and re-layouts  21.9 us (10%)
  between operations  13.5 us (6%)
  matrix products  7.92 us (4%)
  other arithmetic  5.17 us (2%)
    pallas_call x1, Pallas kernels, moe(): pl.pallas_call(moe_kernel, out_shape=jax.ShapeDtypeStruct(hidden.shape, B...  127 us
    all_gather x1, waiting for transfers between devices, on_device(): lax.all_gather(jnp.concatenate((keys, values), axis=0), 'tensor', axis=1,...  37.8 us
    unnamed x7, local copies, waits for them, and re-layouts  12.4 us
    slice x1, local copies, waits for them, and re-layouts, on_device(): key_all, value_all = (both[0], both[1])  6.44 us
    sub x1, matrix products, on_device(): exp_terms = jnp.where(causal, jnp.exp(masked - row_peak), 0.0)  4.89 us
  transfers between devices with their start and end apart: 1, of which 1 were waited for; matrix products, arithmetic and copies ran while one was open for 3% of the time, Pallas kernels for 0%

profile of v1, /device:TPU:1, one launch (start us, length us, event | category | flops | bytes accessed | tf_op | source)
XLA Modules:
  0.0 212.8 jit_solution(822060759870716480)
XLA Ops:
  6.5 0.9 copy.51
  7.5 0.9 copy.50
  8.4 1.0 pad_maximum_fusion
  9.4 0.0 all-gather.2.cloned.1.call-update
  9.4 1.1 reshape_squeeze.11
  10.5 0.7 select_reduce_fusion
  11.2 0.1 copy.65
  11.3 0.1 copy.63
  11.4 0.7 fusion.17
  12.1 0.1 copy.58
  12.2 0.1 copy.61
  12.3 0.1 reduce_window_sum.13
  12.4 0.1 copy.62
  12.5 0.1 copy.59
  12.6 0.1 copy.60
  12.7 0.1 eq.54
  12.8 0.6 broadcast_select_fusion
  13.4 0.7 copy.66.pm
  14.1 0.6 fusion.20.po
  14.7 0.1 iota_compare_fusion
  14.8 0.6 and_select_fusion.go
  15.4 37.8 %all-gather.2.cloned.1.call-done = bf16[2,1024,512]{2,0,1:T(2,128)(2,1)} async-done(((bf16[2,64,512]{2,0,1:T(2,128)(2,1)}), bf16[2,1024,512]{2,0,1:T(2,128)(2,1)}) %all-gather.2.cloned.1.call-update) | async-done | bytes 2097168 | tf_op jit(solution)/shard_map/all_gather | solution.py:371
  53.2 6.4 %fusion.23 = (bf16[1,1024,512]{2,0,1:T(2,128)(2,1)S(1)}, bf16[1,1024,512]{2,0,1:T(2,128)(2,1)}) fusion(bf16[2,1024,512]{2,0,1:T(2,128)(2,1)} %all-gather.2.cloned.1.call-done), kind=kLoop, calls=%fused_computation.33 | loop fusion | bytes 4194304 | tf_op jit(solution)/shard_map/slice | solution.py:372
  59.6 4.6 %copy.73 = bf16[1,1024,512]{1,2,0:T(8,128)(2,1)S(1)} copy(bf16[1,1024,512]{2,0,1:T(2,128)(2,1)} %get-tuple-element.8) | data formatting | bytes 2097152
  64.2 4.3 %copy.74 = bf16[1,1024,512]{1,2,0:T(8,128)(2,1)} copy(bf16[1,1024,512]{2,0,1:T(2,128)(2,1)S(1)} %get-tuple-element.7) | data formatting | bytes 2097152
  68.5 4.9 %fusion.24 = (f32[4,4,64]{2,1,0:T(4,128)S(1)}, f32[4,4,64,1024]{3,2,1,0:T(8,128)}) fusion(pred[64,1024]{1,0:T(8,128)(4,1)S(1)} %iota_compare_fusion, bf16[1024,4,128,1]{0,2,3,1:T(8,128)(2,1)} %bitcast.48, bf16[64,4,4,128]{3,2,1,0:T(4,128)(2,1)S(1)} %reshape_squeeze.11), kind=kOutput, calls=%fused_computation.34 | convolution fusion | flops 273679360 | bytes 5574656 | tf_op jit(solution)/shard_map/sub | solution.py:390
  73.4 3.0 %fusion.6 = f32[64,4,4,128]{3,0,2,1:T(8,128)S(1)} fusion(bf16[1024,4,128,1]{0,2,3,1:T(8,128)(2,1)S(1)} %bitcast.47, f32[4,4,64,1024]{3,2,1,0:T(8,128)} %get-tuple-element.10, f32[4,4,64]{2,1,0:T(4,128)S(1)} %get-tuple-element.9), kind=kOutput, calls=%fused_computation.9 | convolution fusion | flops 270532608 | bytes 5771264 | tf_op jit(solution)/shard_map/kgqt,tkd->qkgd/dot_general | solution.py:392
  76.4 0.3 copy.57
  76.7 0.2 reshape.30
  77.0 0.8 fusion.7.hid
  77.7 126.5 %moe.1 = bf16[64,2048]{1,0:T(8,128)(2,1)} custom-call(bf16[64,2048]{1,0:T(8,128)(2,1)} %fusion.7.hid, bf16[128,64]{1,0:T(8,128)(2,1)} %copy.66.pm, bf16[8,64]{1,0:T(8,128)(2,1)} %fusion.20.po, f32[64,128]{1,0:T(8,128)} %get-tuple-element.5.gm, f32[64,8]{1,0:T(8,128)} %and_select_fusion.go, bf16[1,4096,512]{2,1,0:T(8,128)(2,1)} %wg_any.1, ...), custom_call_target="tpu_custom_call" | custom-call | tf_op jit(solution)/shard_map/moe/pallas_call | solution.py:322
  204.2 1.7 copy.88
  (11 shorter events, 0.1 us)
Async XLA Ops:
  6.5 46.7 %all-gather.2.cloned.1.call-start = ((), (), s32[]{:S(2)}) async-start(), calls=%async_computation | async-start | bytes 2228224 | tf_op jit(solution)/shard_map/all_gather | solution.py:371
  73.4 3.6 %copy-start = (bf16[1,64,2048]{2,1,0:T(8,128)(2,1)S(1)}, bf16[1,64,2048]{2,1,0:T(8,128)(2,1)}, u32[]{:S(2)}) copy-start(bf16[1,64,2048]{2,1,0:T(8,128)(2,1)} %param.12) | copy-start | bytes 786436
Sparse Core Ops, SparseCore 0:
  9.5 43.6 all-gather.1

commit v2 on v1

--- a/solution.py
+++ b/solution.py
@@ -29,15 +29,25 @@
     )
 
 
-def moe_kernel(
-    hid, pm, po, gm, go, wg_any, wu_any, wd_any, out,
+def layer_kernel(
+    q_any, k_any, v_any, res_any, routes, gates, wg_any, wu_any, wd_any, out,
+    qv, res, kv, qs, top, mass, acc, hid, gm, go,
     wg, wu, wd, pk, pov, xr, ovr, xm, xp, inner, yps, ypr, ys, rr, fr, fov, ret, retov,
+    in_sem, kg_s, kg_r, kx_s, kx_r,
     w_sem, d_s, d_r, o_s, o_r, ag_s, ag_r, xs, xrs, yss, yrs, rs_s, rs_r, b_s, b_r, bo_s, bo_r,
 ):
     s, e, t = lax.axis_index("section"), lax.axis_index("expert"), lax.axis_index("tensor")
     z, c = t // 2, t % 2
-    half = hid.shape[1]
+    tokens, half = hid.shape
     cw = half // CHUNKS
+    own_in = [
+        pltpu.make_async_copy(k_any.at[0], kv.at[7, 0, 0], in_sem.at[0]),
+        pltpu.make_async_copy(v_any.at[0], kv.at[7, 0, 1], in_sem.at[1]),
+        pltpu.make_async_copy(q_any.at[0], qv, in_sem.at[2]),
+        pltpu.make_async_copy(res_any.at[0], res, in_sem.at[3]),
+    ]
+    for load in own_in:
+        load.start()
     barrier = pltpu.get_barrier_semaphore()
     for i in range(1, 32):
         other = (s * 2 + c) ^ (i % 4)
@@ -54,15 +64,122 @@
         loads.append(pltpu.make_async_copy(wg_any.at[0, rows, :], wg.at[part], w_sem.at[part]))
         loads.append(pltpu.make_async_copy(wu_any.at[0, rows, :], wu.at[part], w_sem.at[2 + part]))
         loads.append(pltpu.make_async_copy(wd_any.at[0, :, rows], wd.at[part], w_sem.at[4 + part]))
+
+    def slot(way, d):
+        return 7 if d == 0 else 6 if d == 4 else 2 * (d - 1) + way
+
+    partner = (s, e, z * 2 + 1 - c)
+    ring = ((s, e, up * 2 + c), (s, e, down * 2 + c))
+    spread, swap = {}, {}
+    for way in range(2):
+        for d in range(4):
+            for j in range(2) if d < 3 else (way,):
+                spread[way, d, j] = copy_to(
+                    kv.at[slot(way, d), 0, j], kv.at[slot(way, d + 1), 0, j],
+                    kg_s.at[way, 2 * d + j], kg_r.at[way, 2 * d + j], ring[way],
+                )
+    for k in range(8):
+        for j in range(2):
+            swap[k, j] = copy_to(kv.at[k, 0, j], kv.at[k, 1, j], kx_s.at[k, j], kx_r.at[k, j], partner)
+
+    own_in[0].wait()
+    own_in[1].wait()
+    pl.semaphore_wait(barrier, 33)
+    for j in range(2):
+        for way in range(2):
+            spread[way, 0, j].start()
+        swap[7, j].start()
     for load in loads:
         load.start()
 
-    tokens = hid[...]
-    pk[...] = dot(pm[...], tokens).astype(BF).reshape(pk.shape)
-    extra = dot(po[...], tokens)
+    lane = lax.broadcasted_iota(jnp.int32, (tokens, MAIN), 1)
+    first, second = routes[0, :, 0:1], routes[0, :, 1:2]
+    gate0, gate1 = gates[0, :, 0:1], gates[0, :, 1:2]
+    earlier = (
+        lax.broadcasted_iota(jnp.int32, (tokens, tokens), 0) > lax.broadcasted_iota(jnp.int32, (tokens, tokens), 1)
+    ).astype(BF)
+
+    def placed(expert, wanted):
+        is0, is1 = first == expert, second == expert
+        named = jnp.where(is0 | is1, 1.0, 0.0)
+        place = dot(earlier, named.astype(BF))
+        hit = jnp.where(place == wanted.astype(F32), named, 0.0)
+        return hit, hit * (jnp.where(is0, gate0, 0.0) + jnp.where(is1, gate1, 0.0))
+
+    hit_main, gm[...] = placed(lane // (2 * SLOTS), lane % (2 * SLOTS))
+    few = lax.broadcasted_iota(jnp.int32, (tokens, EXPERTS), 1)
+    hit_over, go[...] = placed(few, jnp.full_like(few, 2 * SLOTS))
+
+    own_in[2].wait()
+    kv_heads = qs.shape[0]
+    group = qs.shape[1] // tokens
+    for h in range(kv_heads):
+        for g in range(group):
+            qs[h, tokens * g : tokens * (g + 1), :] = qv[:, HD * (h * group + g) : HD * (h * group + g + 1)]
+    stacked = group * tokens
+    scale = 1.0 / math.sqrt(HD)
+
+    def attend(start, count, bias, fresh):
+        keys = count * 2 * tokens
+
+        def head(h, carry):
+            at = pl.ds(pl.multiple_of(h * HD, HD), HD)
+            k = kv[start : start + count, :, 0, :, at].reshape(keys, HD)
+            v = kv[start : start + count, :, 1, :, at].reshape(keys, HD)
+            scores = lax.dot_general(qs[h], k, (((1,), (1,)), ((), ())), preferred_element_type=F32) * scale + bias
+            peak = jnp.max(scores, axis=1, keepdims=True)
+            if not fresh:
+                peak = jnp.maximum(peak, top[h])
+            terms = jnp.exp(scores - peak)
+            total = jnp.sum(terms, axis=1, keepdims=True)
+            context = dot(terms.astype(BF), v)
+            if not fresh:
+                fade = jnp.exp(top[h] - peak)
+                total = total + mass[h] * fade
+                context = context + acc[h] * fade
+            top[h], mass[h], acc[h] = peak, total, context
+            return carry
+
+        lax.fori_loop(0, kv_heads, head, 0)
+
+    for j in range(2):
+        swap[7, j].wait_recv()
+    row = lax.broadcasted_iota(jnp.int32, (stacked, 2 * tokens), 0) % tokens
+    col = lax.broadcasted_iota(jnp.int32, (stacked, 2 * tokens), 1)
+    attend(7, 1, jnp.where(col <= jnp.where(col < tokens, row, jnp.where(c == 1, 2 * tokens, -1)), 0.0, -1e30), True)
+
+    def ring_bias(d):
+        col = lax.broadcasted_iota(jnp.int32, (1, (2 if d < 4 else 1) * 2 * tokens), 1)
+        return jnp.where(jnp.where(col < 2 * tokens, z - d, z + d - NZ) >= 0, 0.0, -1e30)
+
+    for d in range(1, 5):
+        for j in range(2):
+            for way in range(2) if d < 4 else (j,):
+                spread[way, d - 1, j].wait_recv()
+                if (way, d, j) in spread:
+                    spread[way, d, j].start()
+                swap[slot(way, d), j].start()
+        if d > 1:
+            for way in range(2):
+                for j in range(2):
+                    swap[slot(way, d - 1), j].wait_recv()
+            attend(slot(0, d - 1), 2, ring_bias(d - 1), False)
+    for j in range(2):
+        swap[6, j].wait_recv()
+    attend(6, 1, ring_bias(4), False)
+    own_in[3].wait()
+    for h in range(kv_heads):
+        context = acc[h] / mass[h]
+        for g in range(group):
+            at = slice(HD * (h * group + g), HD * (h * group + g + 1))
+            hid[:, at] = (res[:, at].astype(F32) + context[tokens * g : tokens * (g + 1), :]).astype(BF)
+
+    packed = hid[...]
+    dims = (((0,), (0,)), ((), ()))
+    pk[...] = lax.dot_general(hit_main.astype(BF), packed, dims, preferred_element_type=F32).astype(BF).reshape(pk.shape)
+    extra = lax.dot_general(hit_over.astype(BF), packed, dims, preferred_element_type=F32)
     for j in range(16):
         pov[:, j, :] = extra[:, 128 * j : 128 * (j + 1)]
-    pl.semaphore_wait(barrier, 33)
 
     own = s == c
     sent = []
@@ -110,14 +227,9 @@
     for j in range(16):
         xm[7, MAIN:, 128 * j : 128 * (j + 1)] = ovr[:, j, :].astype(BF)
 
-    def slot(way, d):
-        return 7 if d == 0 else 6 if d == 4 else 2 * (d - 1) + way
-
     def cols(j):
         return pl.ds(cw * j, cw)
 
-    partner = (s, e, z * 2 + 1 - c)
-    ring = ((s, e, up * 2 + c), (s, e, down * 2 + c))
     half_of = ((0, 1), (2, 3))
     gather, share = {}, {}
     for way in range(2):
@@ -300,7 +412,7 @@
         high = weight[...].astype(BF)
         low = (weight[...] - high.astype(F32)).astype(BF)
         total = total + dot(high, part) + dot(low, part)
-    out[...] = total.astype(BF)
+    out[0] = total.astype(BF)
 
     @pl.when(jnp.logical_not(own))
     def _():
@@ -308,23 +420,35 @@
             copy.wait_send()
     for copy in sent:
         copy.wait_send()
-    for table in (gather, share, trade, reduce):
+    for table in (spread, swap, gather, share, trade, reduce):
         for copy in table.values():
             copy.wait_send()
 
 
-def moe(hidden, pm, po, gm, go, w_gate, w_up, w_down):
-    half = hidden.shape[1]
+def on_device(query, keys, values, residual, routes, gates, w_gate, w_up, w_down):
+    _, tokens, half = query.shape
     units = w_gate.shape[2]
+    kv_heads = keys.shape[2] // HD
+    stacked = half // HD // kv_heads * tokens
     vmem = pl.BlockSpec(memory_space=pltpu.VMEM)
     hbm = pl.BlockSpec(memory_space=pl.ANY)
     dma = pltpu.SemaphoreType.DMA
     return pl.pallas_call(
-        moe_kernel,
-        out_shape=jax.ShapeDtypeStruct(hidden.shape, BF),
-        in_specs=[vmem] * 5 + [hbm] * 3,
+        layer_kernel,
+        out_shape=jax.ShapeDtypeStruct(query.shape, BF),
+        in_specs=[hbm] * 4 + [vmem] * 2 + [hbm] * 3,
         out_specs=vmem,
         scratch_shapes=[
+            pltpu.VMEM((tokens, half), BF),
+            pltpu.VMEM((tokens, half), BF),
+            pltpu.VMEM((8, 2, 2, tokens, kv_heads * HD), BF),
+            pltpu.VMEM((kv_heads, stacked, HD), BF),
+            pltpu.VMEM((kv_heads, stacked, 1), F32),
+            pltpu.VMEM((kv_heads, stacked, 1), F32),
+            pltpu.VMEM((kv_heads, stacked, HD), F32),
+            pltpu.VMEM((tokens, half), BF),
+            pltpu.VMEM((tokens, MAIN), F32),
+            pltpu.VMEM((tokens, EXPERTS), F32),
             pltpu.VMEM((2, half, units), BF),
             pltpu.VMEM((2, half, units), BF),
             pltpu.VMEM((2, units, half), BF),
@@ -343,6 +467,7 @@
             pltpu.VMEM((8, 16, 128), F32),
             pltpu.VMEM((16, SLOTS, half), BF),
             pltpu.VMEM((8, 16, 128), F32),
+            dma((4,)), dma((2, 8)), dma((2, 8)), dma((8, 2)), dma((8, 2)),
             dma((6,)), dma((16,)), dma((16,)), dma((8,)), dma((8,)),
             dma((2, 16)), dma((2, 16)), dma((8,)), dma((8,)), dma((4,)), dma((4,)),
             dma((2, 16)), dma((2, 16)), dma((16,)), dma((16,)), dma((8,)), dma((8,)),
@@ -350,49 +475,8 @@
         compiler_params=pltpu.CompilerParams(
             collective_id=1, has_side_effects=True, vmem_limit_bytes=60 * 1024 * 1024
         ),
-        name="moe",
-    )(hidden, pm, po, gm, go, w_gate, w_up, w_down)
-
-
-def tables(picked, gates):
-    hits = picked[:, :, None] == jnp.arange(EXPERTS)
-    named = jnp.any(hits, axis=1)
-    gate = jnp.sum(jnp.where(hits, gates[:, :, None], 0.0), axis=1)
-    place = jnp.cumsum(named.astype(jnp.int32), axis=0) - named.astype(jnp.int32)
-    tokens = picked.shape[0]
-    main = named[:, :, None] & (place[:, :, None] == jnp.arange(2 * SLOTS))
-    gm = jnp.where(main, gate[:, :, None], 0.0).reshape(tokens, MAIN)
-    over = named & (place == 2 * SLOTS)
-    go = jnp.where(over, gate, 0.0)
-    return main.reshape(tokens, MAIN).T.astype(BF), over.T.astype(BF), gm, go
-
-
-def on_device(query, keys, values, residual, routes, gates, w_gate, w_up, w_down):
-    both = lax.all_gather(jnp.concatenate((keys, values), axis=0), "tensor", axis=1, tiled=True)
-    key_all, value_all = both[0], both[1]
-    token_count = query.shape[1]
-    length = key_all.shape[0]
-    half_width = query.shape[2]
-    local_heads = half_width // HD
-    local_kv = keys.shape[2] // HD
-    groups = local_heads // local_kv
-    queries = query[0].reshape(token_count, local_kv, groups, HD)
-    key_heads = key_all.reshape(length, local_kv, HD)
-    value_heads = value_all.reshape(length, local_kv, HD)
-    scores = jnp.einsum(
-        "qkgd,tkd->kgqt", queries, key_heads, preferred_element_type=F32
-    ) / math.sqrt(HD)
-    start_row = lax.axis_index("tensor") * token_count
-    query_positions = start_row + jnp.arange(token_count)
-    causal = query_positions[:, None] >= jnp.arange(length)[None, :]
-    masked = jnp.where(causal, scores, -1e30)
-    row_peak = jnp.max(masked, axis=-1, keepdims=True)
-    exp_terms = jnp.where(causal, jnp.exp(masked - row_peak), 0.0)
-    weights = (exp_terms / jnp.sum(exp_terms, axis=-1, keepdims=True)).astype(BF)
-    context = jnp.einsum("kgqt,tkd->qkgd", weights, value_heads, preferred_element_type=F32)
-    hidden = (residual[0].astype(F32) + context.reshape(token_count, half_width)).astype(BF)
-    pm, po, gm, go = tables(routes[0], gates[0])
-    return moe(hidden, pm, po, gm, go, w_gate, w_up, w_down)[None]
+        name="layer",
+    )(query, keys, values, residual, routes, gates, w_gate, w_up, w_down)
 
 
 def solution(mesh):

time: 213 us -> 158 us (0.74)
  waiting for transfers between devices: 37.8 us -> 0 us
  Pallas kernels: 127 us -> 154 us
  local copies, waits for them, and re-layouts: 21.9 us -> 4.42 us
  between operations: 13.5 us -> 0.01 us
  matrix products: 7.92 us -> 0 us
  other arithmetic: 5.17 us -> 0 us
    all_gather x1 -> x0, waiting for transfers between devices: 37.8 us -> none  [on_device(): lax.all_gather(jnp.concatenate((keys, values), axis=0), 'tensor', axis=1,...]
    pallas_call x1, Pallas kernels: 127 us -> 154 us  [on_device(): pl.pallas_call(layer_kernel, out_shape=jax.ShapeDtypeStruct(query.shape,...]
    unnamed x7 -> x3, local copies, waits for them, and re-layouts: 12.4 us -> 4.42 us
    slice x1 -> x0, local copies, waits for them, and re-layouts: 6.44 us -> none  [on_device(): key_all, value_all = (both[0], both[1])]
    sub x1 -> x0, matrix products: 4.89 us -> none  [on_device(): exp_terms = jnp.where(causal, jnp.exp(masked - row_peak), 0.0)]
    dot_general x1 -> x0, matrix products: 3.03 us -> none  [on_device(): jnp.einsum('kgqt,tkd->qkgd', weights, value_heads, preferred_element_type...]
  transfers between devices with their start and end apart: 1 -> 0, of which waited for: 1 -> 0; matrix products, arithmetic and copies ran while one was open for 3% -> 0% of each run, Pallas kernels for 0% -> 0%
where the time goes in v2:
time: 158 us
  Pallas kernels  154 us (97%)
  local copies, waits for them, and re-layouts  4.42 us (3%)
    pallas_call x1, Pallas kernels, on_device(): pl.pallas_call(layer_kernel, out_shape=jax.ShapeDtypeStruct(query.shape,...  154 us
    unnamed x3, local copies, waits for them, and re-layouts  4.42 us

profile of v2, /device:TPU:1, one launch (start us, length us, event | category | flops | bytes accessed | tf_op | source)
XLA Modules:
  0.0 158.0 jit_solution(13966096444020682572)
XLA Ops:
  0.0 1.4 copy.10.routes
  1.4 1.4 copy.11.gates
  2.7 153.6 %layer.1 = bf16[1,64,2048]{2,1,0:T(8,128)(2,1)} custom-call(bf16[1,64,2048]{2,1,0:T(8,128)(2,1)} %q_any.1, bf16[1,64,512]{2,1,0:T(8,128)(2,1)} %k_any.1, bf16[1,64,512]{2,1,0:T(8,128)(2,1)} %v_any.1, bf16[1,64,2048]{2,1,0:T(8,128)(2,1)} %res_any.1, s32[1,64,2]{2,1,0:T(8,128)} %copy.10.routes, f32[1,64,2]{2,1,0:T(8,128)} %copy.11.gates, ...), custom_call_target="tpu_custom_call" | custom-call | tf_op jit(solution)/shard_map/layer/pallas_call | solution.py:436
  156.3 1.7 %copy.13 = bf16[1,64,2048]{2,1,0:T(8,128)(2,1)} copy(bf16[1,64,2048]{2,1,0:T(8,128)(2,1)} %layer.1) | data formatting | bytes 524288

commit v3 on v0

v3 whole, which is shorter than its diff:
```python
import math

import jax
import jax.numpy as jnp
from jax import lax
from jax.experimental import pallas as pl
from jax.experimental.pallas import tpu as pltpu
from jax.sharding import PartitionSpec as P

HD = 128
EXPERTS = 8
NZ = 8
SLOTS = 8
MAIN = 2 * SLOTS * EXPERTS
ROWS = MAIN + EXPERTS
CHUNKS = 4
WIDE = 768
RING = 256
FAR = (0, 2, 4, 6, 5, 3, 1)
MESH = pl.DeviceIdType.MESH
BF = jnp.bfloat16
F32 = jnp.float32


def dot(a, b):
    return jnp.dot(a, b, preferred_element_type=F32)


def dot_rows(a, b):
    return lax.dot_general(a, b, (((0,), (0,)), ((), ())), preferred_element_type=F32)


def copy_to(src, dst, send, recv, device):
    return pltpu.make_async_remote_copy(
        src_ref=src, dst_ref=dst, send_sem=send, recv_sem=recv, device_id=device, device_id_type=MESH
    )


def layer_kernel(
    q_any, k_any, v_any, res_any, routes, gates, wg_any, wu_any, wd_any, out,
    qv, res, kv, qs, top, mass, acc, hid, rz, hits, overs, high, low, ohigh, olow, hz,
    wg, wu, wd, pk, pov, ovr, pw, pvw, ovw, xm, xp, partial, inner, yps, ypr, ys, rr, fov, ret, retov,
    rb, pvb, ovb, cz, rc,
    in_sem, rz_s, rz_r, kg_s, kg_r, kx_s, kx_r, hz_s, hz_r, dw_s, dw_r, ow_s, ow_r,
    w_sem, d_s, d_r, o_s, o_r, ag_s, ag_r, xs, xrs, yss, yrs, rs_s, rs_r, b_s, b_r, bo_s, bo_r,
    bw_s, bw_r, vw_s, vw_r, cr_s, cr_r,
):
    s, e, t = lax.axis_index("section"), lax.axis_index("expert"), lax.axis_index("tensor")
    z, c = t // 2, t % 2
    tokens, half = hid.shape
    cw = half // CHUNKS
    kv_heads = qs.shape[0]
    own_in = []
    for h in range(kv_heads):
        at = pl.ds(HD * h, HD)
        own_in.append(pltpu.make_async_copy(k_any.at[0, :, at], kv.at[7, 0, h, 0], in_sem.at[2 * h]))
        own_in.append(pltpu.make_async_copy(v_any.at[0, :, at], kv.at[7, 0, h, 1], in_sem.at[2 * h + 1]))
    queries_in = pltpu.make_async_copy(q_any.at[0], qv, in_sem.at[8])
    residual_in = pltpu.make_async_copy(res_any.at[0], res, in_sem.at[9])
    own_in += [queries_in, residual_in]
    for load in own_in:
        load.start()
    barrier = pltpu.get_barrier_semaphore()
    for i in range(1, 32):
        other = (s * 2 + c) ^ (i % 4)
        pl.semaphore_signal(
            barrier, inc=1, device_id=(other // 2, (e + i // 4) % 8, z * 2 + other % 2), device_id_type=MESH
        )
    up, down = (z + 1) % NZ, (z + NZ - 1) % NZ
    for k in range(1, NZ):
        pl.semaphore_signal(barrier, inc=1, device_id=(s, e, ((z + k) % NZ) * 2 + c), device_id_type=MESH)
    rz[7] = jnp.zeros(rz.shape[1:], F32)
    rz[7, 0:2, 0:tokens] = routes[...].astype(F32)
    rz[7, 2:4, 0:tokens] = gates[...]
    loads = []
    for part in range(2):
        h = (c + part) % 2
        rows = pl.ds(pl.multiple_of(h * half, half), half)
        loads.append(pltpu.make_async_copy(wg_any.at[0, rows, :], wg.at[part], w_sem.at[part]))
        loads.append(pltpu.make_async_copy(wu_any.at[0, rows, :], wu.at[part], w_sem.at[2 + part]))
        loads.append(pltpu.make_async_copy(wd_any.at[0, :, rows], wd.at[part], w_sem.at[4 + part]))

    def slot(way, d):
        return 7 if d == 0 else 6 if d == 4 else 2 * (d - 1) + way

    partner = (s, e, z * 2 + 1 - c)
    ring = ((s, e, up * 2 + c), (s, e, down * 2 + c))

    def spread(way, d, h):
        return copy_to(
            kv.at[slot(way, d), 0, h], kv.at[slot(way, d + 1), 0, h],
            kg_s.at[way, 4 * d + h], kg_r.at[way, 4 * d + h], ring[way],
        )

    def swap(k, h):
        return copy_to(kv.at[k, 0, h], kv.at[k, 1, h], kx_s.at[k, h], kx_r.at[k, h], partner)

    tell = [
        copy_to(rz.at[7], rz.at[FAR[k - 1]], rz_s.at[k - 1], rz_r.at[k - 1], (s, e, ((z + k) % NZ) * 2 + c))
        for k in range(1, NZ)
    ]
    for load in own_in[:8]:
        load.wait()
    pl.semaphore_wait(barrier, 38)
    for h in range(kv_heads):
        for way in range(2):
            spread(way, 0, h).start()
        swap(7, h).start()
    for copy in tell:
        copy.start()
    for load in loads:
        load.start()

    earlier = (
        lax.broadcasted_iota(jnp.int32, (tokens, tokens), 0) < lax.broadcasted_iota(jnp.int32, (tokens, tokens), 1)
    ).astype(BF)

    line = lax.broadcasted_iota(jnp.int32, (MAIN, tokens), 0)
    few = lax.broadcasted_iota(jnp.int32, (EXPERTS, tokens), 0)

    def placed(k, expert, wanted, hit_ref, high_ref, low_ref):
        is0, is1 = (rz[k, n : n + 1, 0:tokens] == expert.astype(F32) for n in range(2))
        gate0, gate1 = (rz[k, n : n + 1, 0:tokens] for n in (2, 3))
        named = jnp.where(is0 | is1, 1.0, 0.0)
        place = dot(named.astype(BF), earlier)
        hit = jnp.where(place == wanted.astype(F32), named, 0.0)
        weight = hit * (jnp.where(is0, gate0, 0.0) + jnp.where(is1, gate1, 0.0))
        top_part = weight.astype(BF)
        hit_ref[k] = hit.astype(BF)
        high_ref[k] = top_part
        low_ref[k] = (weight - top_part.astype(F32)).astype(BF)

    def slot_tables(k):
        placed(k, line // (2 * SLOTS), line % (2 * SLOTS), hits, high, low)
        placed(k, few, jnp.full_like(few, 2 * SLOTS), overs, ohigh, olow)

    slot_tables(7)
    queries_in.wait()
    group = qs.shape[1] // tokens
    for h in range(kv_heads):
        for g in range(group):
            qs[h, tokens * g : tokens * (g + 1), :] = qv[:, HD * (h * group + g) : HD * (h * group + g + 1)]
    stacked = group * tokens
    scale = math.log2(math.e) / math.sqrt(HD)

    def attend(start, count, bias, fresh, h):
        keys = count * 2 * tokens
        k = kv[start : start + count, :, h, 0].reshape(keys, HD)
        v = kv[start : start + count, :, h, 1].reshape(keys, HD)
        scores = lax.dot_general(qs[h], k, (((1,), (1,)), ((), ())), preferred_element_type=F32) * scale + bias
        peak = jnp.max(scores, axis=1, keepdims=True)
        if not fresh:
            peak = jnp.maximum(peak, top[h])
        terms = jnp.exp2(scores - peak).astype(BF)
        both = dot(terms, jnp.concatenate([v, jnp.ones_like(v)], axis=1))
        context, total = both[:, :HD], both[:, HD:]
        if not fresh:
            fade = jnp.exp2(top[h] - peak)
            total = total + mass[h] * fade
            context = context + acc[h] * fade
        top[h], mass[h], acc[h] = peak, total, context

    row = lax.broadcasted_iota(jnp.int32, (stacked, 2 * tokens), 0) % tokens
    col = lax.broadcasted_iota(jnp.int32, (stacked, 2 * tokens), 1)
    diagonal = jnp.where(col <= jnp.where(col < tokens, row, jnp.where(c == 1, 2 * tokens, -1)), 0.0, -1e30)

    def ring_bias(d):
        col = lax.broadcasted_iota(jnp.int32, (1, (2 if d < 4 else 1) * 2 * tokens), 1)
        return jnp.where(jnp.where(col < 2 * tokens, z - d, z + d - NZ) >= 0, 0.0, -1e30)

    def first_step(h, carry):
        swap(7, h).wait_recv()
        attend(7, 1, diagonal, True, h)
        return carry

    lax.fori_loop(0, kv_heads, first_step, 0)
    for d in range(1, 4):
        bias = ring_bias(d - 1) if d > 1 else None

        def ring_step(h, carry, d=d, bias=bias):
            for way in range(2):
                spread(way, d - 1, h).wait_recv()
                if d < 3:
                    spread(way, d, h).start()
                else:
                    pl.when(h // 2 == way)(spread(way, d, h).start)
                swap(slot(way, d), h).start()
            if d > 1:
                for way in range(2):
                    swap(slot(way, d - 1), h).wait_recv()
                attend(slot(0, d - 1), 2, bias, False, h)
            return carry

        lax.fori_loop(0, kv_heads, ring_step, 0)
    bias = ring_bias(3)

    def last_step(h, carry):
        for way in range(2):
            swap(slot(way, 3), h).wait_recv()
        attend(slot(0, 3), 2, bias, False, h)
        return carry

    bias4 = ring_bias(4)
    for copy in tell:
        copy.wait_recv()
    for k in range(7):
        slot_tables(k)
    for h in range(2):
        last_step(h, 0)
        for way in range(2):
            spread(way, 3, 2 * way + h).wait_recv()
            swap(6, 2 * way + h).start()
    residual_in.wait()

    own = s == c
    wide = WIDE
    rings = (half - wide) // RING
    ring_half = (tuple(range((rings + 1) // 2)), tuple(range((rings + 1) // 2, rings)))
    hw = half // kv_heads
    sent, own_sent = [], []

    def ring_cols(j):
        return pl.ds(wide + RING * j, RING)

    def send(copy, i, same):
        if i == 0 and same:
            pl.when(jnp.logical_not(own))(copy.start)
            own_sent.append(copy)
        else:
            copy.start()
            sent.append(copy)

    def receive(copy, i, same):
        if i == 0 and same:
            pl.when(jnp.logical_not(own))(copy.wait_recv)
        else:
            copy.wait_recv()

    def source_rows(ef, cf):
        return pl.ds(pl.multiple_of((ef * 2 + cf) * SLOTS, SLOTS), SLOTS)

    carry_on = {}
    for way in range(2):
        for d in range(4):
            for j in range(2) if d < 3 else (way,):
                at = pl.ds(wide // 2 * j, wide // 2)
                carry_on[way, d, j] = copy_to(
                    hz.at[slot(way, d), :, at], hz.at[slot(way, d + 1), :, at],
                    hz_s.at[way, 2 * d + j], hz_r.at[way, 2 * d + j], ring[way],
                )

    for h in range(kv_heads):
        swap(6, h).wait_recv()
        if h >= 2:
            last_step(h, 0)
        attend(6, 1, bias4, False, h)
        context = acc[h] / mass[h]
        for g in range(group):
            at = slice(HD * (h * group + g), HD * (h * group + g + 1))
            hid[:, at] = (res[:, at].astype(F32) + context[tokens * g : tokens * (g + 1), :]).astype(BF)
        from_col = hw * h
        if from_col < wide:
            to_col = min(wide, from_col + hw)
            hz[7, :, from_col:to_col] = hid[:, from_col:to_col]
            for j in range(2):
                if from_col < wide // 2 * (j + 1) <= to_col:
                    for way in range(2):
                        carry_on[way, 0, j].start()
        if h == 0:
            continue
        a = h - 1
        from_col = max(from_col, wide)
        width = hw * (h + 1) - from_col
        piece = hid[:, from_col : from_col + width]
        part = pl.ds(from_col - wide, width)
        pk[:, :, part] = dot(hits[7], piece).astype(BF).reshape(16, SLOTS, width)
        extra = dot(overs[7], piece)
        for q in range(width // 128):
            pov[a, :, q, :] = extra[:, 128 * q : 128 * (q + 1)]
        land = pl.ds(from_col, width)

        @pl.when(own)
        def _():
            xm[7, source_rows(e, c), land] = pk[e * 2 + s, :, part]
            ovr[a, e] = pov[a, e]

        for i in range(8):
            ed = (e + i) % 8
            for k in (1, 0):
                sd = (s + k) % 2
                send(
                    copy_to(
                        pk.at[ed * 2 + sd, :, part], xm.at[7, source_rows(e, c), land],
                        d_s.at[a, i * 2 + k], d_r.at[a, e * 2 + c], (sd, ed, z * 2 + s),
                    ), i, k == 0,
                )
            send(copy_to(pov.at[a, ed], ovr.at[a, e], o_s.at[a, i], o_r.at[a, e], (c, ed, z * 2 + s)), i, True)

    groups = ((7, 1), (0, 2), (2, 2), (4, 2), (6, 1))

    def send_wide(w):
        start, count = groups[w]
        for p in range(count):
            tokens_of = hz[start + p]
            pw[w, :, p] = dot(hits[start + p], tokens_of).astype(BF).reshape(16, SLOTS, wide)
            extra = dot(overs[start + p], tokens_of)
            for q in range(wide // 128):
                pvw[w, :, p, q, :] = extra[:, 128 * q : 128 * (q + 1)]
        many = pl.ds(0, count)
        slots = pl.ds(start, count)
        at = pl.ds(0, wide)

        @pl.when(own)
        def _():
            xm[slots, source_rows(e, c), at] = pw[w, e * 2 + s, many]
            ovw[w, e, many] = pvw[w, e, many]

        for i in range(8):
            ed = (e + i) % 8
            for k in (1, 0):
                sd = (s + k) % 2
                send(
                    copy_to(
                        pw.at[w, ed * 2 + sd, many], xm.at[slots, source_rows(e, c), at],
                        dw_s.at[w, i * 2 + k], dw_r.at[w, e * 2 + c], (sd, ed, z * 2 + s),
                    ), i, k == 0,
                )
            send(
                copy_to(pvw.at[w, ed, many], ovw.at[w, e, many], ow_s.at[w, i], ow_r.at[w, e], (c, ed, z * 2 + s)),
                i, True,
            )

    def receive_wide(w):
        start, count = groups[w]
        many = pl.ds(0, count)
        slots = pl.ds(start, count)
        at = pl.ds(0, wide)
        for i in range(8):
            ef = (e + 8 - i) % 8
            for k in range(2):
                cf = (c + k) % 2
                receive(
                    copy_to(
                        pw.at[w, 0, many], xm.at[slots, source_rows(ef, cf), at],
                        dw_s.at[w, 0], dw_r.at[w, ef * 2 + cf], (c, ef, z * 2 + cf),
                    ), i, k == 0,
                )
            receive(
                copy_to(pvw.at[w, 0, many], ovw.at[w, ef, many], ow_s.at[w, 0], ow_r.at[w, ef], (c, ef, z * 2 + s)),
                i, True,
            )
        for p in range(count):
            for q in range(wide // 128):
                xm[start + p, MAIN:, 128 * q : 128 * (q + 1)] = ovw[w, :, p, q, :].astype(BF)
            share[start + p, 0].start()

    def carry(d):
        for j in range(2):
            for way in range(2) if d < 4 else (j,):
                carry_on[way, d - 1, j].wait_recv()
                if (way, d, j) in carry_on:
                    carry_on[way, d, j].start()

    def cols(j):
        return pl.ds(cw * j, cw)

    half_of = ((0, 1), (2, 3))
    gather, share = {}, {}
    split = wide + 3 * RING
    parts = ((0, wide), (wide, split), (split, half))
    for way in range(2):
        for d in range(4):
            for j in range(rings) if d < 3 else ring_half[way]:
                n = d * rings + j
                gather[way, d, j] = copy_to(
                    xm.at[slot(way, d), :, ring_cols(j)], xm.at[slot(way, d + 1), :, ring_cols(j)],
                    ag_s.at[way, n], ag_r.at[way, n], ring[way],
                )
    for k in range(8):
        for n, (begin, end) in enumerate(parts):
            at = pl.ds(begin, end - begin)
            share[k, n] = copy_to(xm.at[k, :, at], xp.at[k, :, at], xs.at[k, n], xrs.at[k, n], partner)

    def trade(g, j):
        at = pl.ds(pl.multiple_of(j * cw, cw), cw)
        pair = pl.ds(2 * g - 2, 2)
        return copy_to(yps.at[pair, :, at], ypr.at[pair, :, at], yss.at[g - 1, j], yrs.at[g - 1, j], partner)

    def hidden_units(g, first, last):
        def piece(k, carry):
            at = pl.ds(pl.multiple_of(k * 256, 256), 256)
            left = xm[2 * g - 2 : 2 * g].reshape(2 * ROWS, half)
            right = xp[2 * g - 2 : 2 * g].reshape(2 * ROWS, half)
            gate = dot(left, wg[0, :, at]) + dot(right, wg[1, :, at])
            lift = dot(left, wu[0, :, at]) + dot(right, wu[1, :, at])
            inner[pl.ds((2 * g - 2) * ROWS, 2 * ROWS), at] = (gate / (1.0 + jnp.exp(-gate)) * lift).astype(BF)
            return carry

        lax.fori_loop(first, last, piece, 0)

    def units_part(g, n, fresh, done):
        begin, end = parts[n]
        at_k = pl.ds(begin, end - begin)

        def piece(k, carry):
            at = pl.ds(pl.multiple_of(k * 256, 256), 256)
            left = xm[2 * g - 2 : 2 * g, :, at_k].reshape(2 * ROWS, end - begin)
            right = xp[2 * g - 2 : 2 * g, :, at_k].reshape(2 * ROWS, end - begin)
            gate = dot(left, wg[0, at_k, at]) + dot(right, wg[1, at_k, at])
            lift = dot(left, wu[0, at_k, at]) + dot(right, wu[1, at_k, at])
            if not fresh:
                gate, lift = gate + partial[0, :, at], lift + partial[1, :, at]
            if done:
                inner[pl.ds((2 * g - 2) * ROWS, 2 * ROWS), at] = (gate / (1.0 + jnp.exp(-gate)) * lift).astype(BF)
            else:
                partial[0, :, at], partial[1, :, at] = gate, lift
            return carry

        lax.fori_loop(0, 2, piece, 0)

    def down_out(g):
        rows = inner[pl.ds((2 * g - 2) * ROWS, 2 * ROWS), :]

        def theirs(j, carry):
            at = pl.ds(pl.multiple_of(j * cw, cw), cw)
            yps[pl.ds(2 * g - 2, 2), :, at] = dot(rows, wd[1, :, at]).astype(BF).reshape(2, ROWS, cw)
            trade(g, j).start()
            return carry

        lax.fori_loop(0, CHUNKS, theirs, 0)

    def down_own(g):
        rows = inner[pl.ds((2 * g - 2) * ROWS, 2 * ROWS), :]

        def mine(j, carry):
            trade(g, j).wait_recv()
            at = pl.ds(pl.multiple_of(j * cw, cw), cw)
            both = dot(rows, wd[0, :, at]).reshape(2, ROWS, cw) + ypr[pl.ds(2 * g - 2, 2), :, at].astype(F32)
            ys[pl.ds(2 * g - 2, 2), :, at] = both.astype(BF)
            return carry

        lax.fori_loop(0, CHUNKS, mine, 0)

    reduce, link = {}, {}
    for way in range(2):
        for d in range(1, 5):
            target = slot(1 - way, d)
            for j in range(rings) if d < 4 else ring_half[way]:
                n = (d - 1) * rings + j
                reduce[way, d, j] = copy_to(
                    ys.at[target, :, ring_cols(j)], rr.at[way, d - 1, :, pl.ds(RING * j, RING)],
                    rs_s.at[way, n], rs_r.at[way, n], ring[way],
                )
            for j in range(2) if d < 4 else (way,):
                at = pl.ds(wide // 2 * j, wide // 2)
                link[way, d, j] = copy_to(
                    cz.at[target, :, at], rc.at[way, d - 1, :, at],
                    cr_s.at[way, 2 * (d - 1) + j], cr_r.at[way, 2 * (d - 1) + j], ring[way],
                )

    def pass_on(way, d, j, add):
        if add:
            reduce[way, d + 1, j].wait_recv()
            k = slot(1 - way, d)
            total = ys[k, :, ring_cols(j)].astype(F32) + rr[way, d, :, pl.ds(RING * j, RING)].astype(F32)
            ys[k, :, ring_cols(j)] = total.astype(BF)
        reduce[way, d, j].start()

    def both_ways(d, lists, add):
        for n in range(max(len(lists[0]), len(lists[1]))):
            for way in range(2):
                if n < len(lists[way]):
                    pass_on(way, d, lists[way][n], add)

    def chain(d):
        for j in range(2):
            at = pl.ds(wide // 2 * j, wide // 2)
            for way in range(2):
                if (way, d, j) in link:
                    if (way, d + 1, j) in link:
                        link[way, d + 1, j].wait_recv()
                        k = slot(1 - way, d)
                        cz[k, :, at] = (cz[k, :, at].astype(F32) + rc[way, d, :, at].astype(F32)).astype(BF)
                    link[way, d, j].start()

    def weigh(k, rows, extra):
        return (
            dot_rows(high[k], rows) + dot_rows(low[k], rows) + dot_rows(ohigh[k], extra) + dot_rows(olow[k], extra)
        )

    def send_back(w):
        start, count = groups[w]
        many, slots, at = pl.ds(0, count), pl.ds(start, count), pl.ds(0, wide)
        for p in range(count):
            tail = ys[start + p, MAIN:, at].astype(F32)
            for q in range(wide // 128):
                pvb[w, :, p, q, :] = tail[:, 128 * q : 128 * (q + 1)]

        @pl.when(own)
        def _():
            rb[w, e * 2 + s, many] = ys[slots, source_rows(e, c), at]
            ovb[w, e, many] = pvb[w, e, many]

        for i in range(8):
            ed = (e + i) % 8
            for k in (1, 0):
                cd = (c + k) % 2
                send(
                    copy_to(
                        ys.at[slots, source_rows(ed, cd), at], rb.at[w, e * 2 + s, many],
                        bw_s.at[w, i * 2 + k], bw_r.at[w, e * 2 + s], (c, ed, z * 2 + cd),
                    ), i, k == 0,
                )
            send(
                copy_to(pvb.at[w, ed, many], ovb.at[w, e, many], vw_s.at[w, i], vw_r.at[w, e], (c, ed, z * 2 + s)),
                i, True,
            )

    def receive_back(w):
        start, count = groups[w]
        many, slots, at = pl.ds(0, count), pl.ds(start, count), pl.ds(0, wide)
        for i in range(8):
            ef = (e + 8 - i) % 8
            for k in range(2):
                sf = (s + k) % 2
                receive(
                    copy_to(
                        ys.at[slots, source_rows(0, 0), at], rb.at[w, ef * 2 + sf, many],
                        bw_s.at[w, 0], bw_r.at[w, ef * 2 + sf], (sf, ef, z * 2 + s),
                    ), i, k == 0,
                )
            receive(
                copy_to(pvb.at[w, 0, many], ovb.at[w, ef, many], vw_s.at[w, 0], vw_r.at[w, ef], (c, ef, z * 2 + s)),
                i, True,
            )
        totals = []
        for p in range(count):
            extra = jnp.concatenate([ovb[w, :, p, q, :] for q in range(wide // 128)], axis=1).astype(BF)
            totals.append(weigh(start + p, rb[w, :, p].reshape(MAIN, wide), extra))
            if w > 0:
                cz[start + p] = totals[p].astype(BF)
        return totals[0]

    send_wide(0)
    carry(1)
    send_wide(1)
    for a in range(3):
        from_col = max(wide, hw * (a + 1))
        width = hw * (a + 2) - from_col
        land = pl.ds(from_col, width)
        part = pl.ds(from_col - wide, width)
        for i in range(8):
            ef = (e + 8 - i) % 8
            for k in range(2):
                cf = (c + k) % 2
                receive(
                    copy_to(
                        pk.at[0, :, part], xm.at[7, source_rows(ef, cf), land],
                        d_s.at[a, 0], d_r.at[a, ef * 2 + cf], (c, ef, z * 2 + cf),
                    ), i, k == 0,
                )
            receive(copy_to(pov.at[a, 0], ovr.at[a, ef], o_s.at[a, 0], o_r.at[a, ef], (c, ef, z * 2 + s)), i, True)
        for q in range(width // 128):
            at = from_col + 128 * q
            xm[7, MAIN:, at : at + 128] = ovr[a, :, q, :].astype(BF)
        for j in range((from_col - wide) // RING, (from_col - wide + width) // RING):
            for way in range(2):
                gather[way, 0, j].start()
        if a == 1:
            carry(2)
    share[7, 1].start()
    share[7, 2].start()
    send_wide(2)
    carry(3)
    send_wide(3)
    for load in loads:
        load.wait()

    receive_wide(0)

    def shared(k):
        for n in range(3):
            share[k, n].wait_recv()

    for d in range(1, 4):
        if d > 1:
            receive_wide(d - 1)
            for way in range(2):
                shared(slot(way, d - 1))
        for j in range(rings):
            for way in range(2):
                gather[way, d - 1, j].wait_recv()
                if (way, d, j) in gather:
                    gather[way, d, j].start()
                if j in (2, rings - 1):
                    share[slot(way, d), 1 + j // 3].start()
            if d == 1 and j == 1:
                carry(4)
                send_wide(4)
            if d > 1 and j in (1, 3):
                hidden_units(d - 1, j // 2, j // 2 + 1)
            if d == 3 and j == 2:
                receive_wide(3)
            if d == 3 and j == 3:
                for way in range(2):
                    share[slot(way, 3), 1].wait_recv()
                units_part(3, 1, True, False)
    receive_wide(4)
    for way in range(2):
        share[slot(way, 3), 2].wait_recv()
    units_part(3, 2, False, False)
    for way in range(2):
        share[slot(way, 3), 0].wait_recv()
    units_part(3, 0, False, True)
    down_out(3)
    down_out(2)
    for way in range(2):
        for j in ring_half[way]:
            gather[way, 3, j].wait_recv()
    share[6, 1].start()
    share[6, 2].start()
    down_own(3)

    swapped = (ring_half[1], ring_half[0])
    orders = tuple(b + a for a, b in zip(ring_half, swapped))
    lasts = (orders[0], (0, 3, 4, 1, 2))
    both_ways(3, swapped, False)
    send_back(3)
    down_own(2)
    shared(6)
    shared(7)
    hidden_units(4, 0, 1)
    both_ways(2, swapped, True)
    hidden_units(4, 1, 2)
    down_out(4)
    down_own(4)
    both_ways(4, ring_half, False)
    send_back(4)
    send_back(2)
    down_out(1)
    receive_back(3)
    both_ways(3, ring_half, True)
    receive_back(4)
    chain(4)
    down_own(1)
    send_back(1)
    send_back(0)
    both_ways(2, ring_half, True)
    chain(3)
    receive_back(2)
    both_ways(1, tuple(o[:2] for o in lasts), True)
    chain(2)
    receive_back(1)
    both_ways(1, tuple(o[2:4] for o in lasts), True)
    chain(1)
    both_ways(1, tuple(o[4:] for o in lasts), True)

    pieces = ((3, 2), (0, 2), (2, 1))
    for a, (j, count) in enumerate(pieces):
        width = count * RING
        for n in range(j, j + count):
            for way in range(2):
                reduce[way, 1, n].wait_recv()
        land, part = pl.ds(wide + RING * j, width), pl.ds(RING * j, width)
        total = (
            ys[7, :, land].astype(F32) + rr[0, 0, :, part].astype(F32) + rr[1, 0, :, part].astype(F32)
        ).astype(BF)
        ys[7, :, land] = total
        tail = total[MAIN:].astype(F32)
        for q in range(width // 128):
            fov[a, :, q, :] = tail[:, 128 * q : 128 * (q + 1)]

        @pl.when(own)
        def _():
            ret[e * 2 + s, :, part] = ys[7, source_rows(e, c), land]
            retov[a, e] = fov[a, e]

        for i in range(8):
            ed = (e + i) % 8
            for k in (1, 0):
                cd = (c + k) % 2
                send(
                    copy_to(
                        ys.at[7, source_rows(ed, cd), land], ret.at[e * 2 + s, :, part],
                        b_s.at[a, i * 2 + k], b_r.at[a, e * 2 + s], (c, ed, z * 2 + cd),
                    ), i, k == 0,
                )
            send(copy_to(fov.at[a, ed], retov.at[a, e], bo_s.at[a, i], bo_r.at[a, e], (c, ed, z * 2 + s)), i, True)

    total = receive_back(0)
    for way in range(2):
        for j in range(2):
            link[way, 1, j].wait_recv()
        total = total + rc[way, 0].astype(F32)
    out[0, :, 0:wide] = (hid[:, 0:wide].astype(F32) + total).astype(BF)

    for a, (j, count) in enumerate(pieces):
        width = count * RING
        land, part = pl.ds(wide + RING * j, width), pl.ds(RING * j, width)
        for i in range(8):
            ef = (e + 8 - i) % 8
            for k in range(2):
                sf = (s + k) % 2
                receive(
                    copy_to(
                        ys.at[7, source_rows(0, 0), land], ret.at[ef * 2 + sf, :, part],
                        b_s.at[a, 0], b_r.at[a, ef * 2 + sf], (sf, ef, z * 2 + s),
                    ), i, k == 0,
                )
            receive(copy_to(fov.at[a, 0], retov.at[a, ef], bo_s.at[a, 0], bo_r.at[a, ef], (c, ef, z * 2 + s)), i, True)
        extra = jnp.concatenate([retov[a, :, q, :] for q in range(width // 128)], axis=1).astype(BF)
        total = weigh(7, ret[:, :, part].reshape(MAIN, width), extra)
        out[0, :, land] = (hid[:, land].astype(F32) + total).astype(BF)

    @pl.when(jnp.logical_not(own))
    def _():
        for copy in own_sent:
            copy.wait_send()
    for copy in sent:
        copy.wait_send()
    for way in range(2):
        for d in range(4):
            for h in range(kv_heads) if d < 3 else half_of[way]:
                spread(way, d, h).wait_send()
    for k in range(8):
        for h in range(kv_heads):
            swap(k, h).wait_send()
    for copy in tell:
        copy.wait_send()
    for g in range(1, 5):
        for j in range(CHUNKS):
            trade(g, j).wait_send()
    for table in (carry_on, gather, share, reduce, link):
        for copy in table.values():
            copy.wait_send()


def on_device(query, keys, values, residual, routes, gates, w_gate, w_up, w_down):
    _, tokens, half = query.shape
    units = w_gate.shape[2]
    kv_heads = keys.shape[2] // HD
    stacked = half // HD // kv_heads * tokens
    vmem = pl.BlockSpec(memory_space=pltpu.VMEM)
    hbm = pl.BlockSpec(memory_space=pl.ANY)
    dma = pltpu.SemaphoreType.DMA
    return pl.pallas_call(
        layer_kernel,
        out_shape=jax.ShapeDtypeStruct(query.shape, BF),
        in_specs=[hbm] * 4 + [vmem] * 2 + [hbm] * 3,
        out_specs=vmem,
        scratch_shapes=[
            pltpu.VMEM((tokens, half), BF),
            pltpu.VMEM((tokens, half), BF),
            pltpu.VMEM((8, 2, kv_heads, 2, tokens, HD), BF),
            pltpu.VMEM((kv_heads, stacked, HD), BF),
            pltpu.VMEM((kv_heads, stacked, 1), F32),
            pltpu.VMEM((kv_heads, stacked, HD), F32),
            pltpu.VMEM((kv_heads, stacked, HD), F32),
            pltpu.VMEM((tokens, half), BF),
            pltpu.VMEM((8, 8, 128), F32),
            pltpu.VMEM((8, MAIN, tokens), BF),
            pltpu.VMEM((8, EXPERTS, tokens), BF),
            pltpu.VMEM((8, MAIN, tokens), BF),
            pltpu.VMEM((8, MAIN, tokens), BF),
            pltpu.VMEM((8, EXPERTS, tokens), BF),
            pltpu.VMEM((8, EXPERTS, tokens), BF),
            pltpu.VMEM((8, tokens, WIDE), BF),
            pltpu.VMEM((2, half, units), BF),
            pltpu.VMEM((2, half, units), BF),
            pltpu.VMEM((2, units, half), BF),
            pltpu.VMEM((16, SLOTS, half - WIDE), BF),
            pltpu.VMEM((3, 8, 8, 128), F32),
            pltpu.VMEM((3, 8, 8, 128), F32),
            pltpu.VMEM((5, 16, 2, SLOTS, WIDE), BF),
            pltpu.VMEM((5, 8, 2, 8, 128), F32),
            pltpu.VMEM((5, 8, 2, 8, 128), F32),
            pltpu.VMEM((8, ROWS, half), BF),
            pltpu.VMEM((8, ROWS, half), BF),
            pltpu.VMEM((2, 2 * ROWS, units), F32),
            pltpu.VMEM((8 * ROWS, units), BF),
            pltpu.VMEM((8, ROWS, half), BF),
            pltpu.VMEM((8, ROWS, half), BF),
            pltpu.VMEM((8, ROWS, half), BF),
            pltpu.VMEM((2, 4, ROWS, half - WIDE), BF),
            pltpu.VMEM((3, 8, 8, 128), F32),
            pltpu.VMEM((16, SLOTS, half - WIDE), BF),
            pltpu.VMEM((3, 8, 8, 128), F32),
            pltpu.VMEM((5, 16, 2, SLOTS, WIDE), BF),
            pltpu.VMEM((5, 8, 2, 8, 128), F32),
            pltpu.VMEM((5, 8, 2, 8, 128), F32),
            pltpu.VMEM((8, tokens, WIDE), BF),
            pltpu.VMEM((2, 4, tokens, WIDE), BF),
            dma((10,)), dma((7,)), dma((7,)), dma((2, 16)), dma((2, 16)), dma((8, 4)), dma((8, 4)),
            dma((2, 8)), dma((2, 8)), dma((5, 16)), dma((5, 16)), dma((5, 8)), dma((5, 8)),
            dma((6,)), dma((3, 16)), dma((3, 16)), dma((3, 8)), dma((3, 8)),
            dma((2, 32)), dma((2, 32)), dma((8, 3)), dma((8, 3)), dma((4, 4)), dma((4, 4)),
            dma((2, 32)), dma((2, 32)), dma((3, 16)), dma((3, 16)), dma((3, 8)), dma((3, 8)),
            dma((5, 16)), dma((5, 16)), dma((5, 8)), dma((5, 8)), dma((2, 8)), dma((2, 8)),
        ],
        compiler_params=pltpu.CompilerParams(
            collective_id=1, has_side_effects=True, vmem_limit_bytes=60 * 1024 * 1024
        ),
        name="layer",
    )(query, keys, values, residual, routes[0].T, gates[0].T, w_gate, w_up, w_down)


def solution(mesh):
    return jax.shard_map(
        on_device,
        mesh=mesh,
        in_specs=(
            P("expert", "tensor", "section"),
            P("expert", "tensor", "section"),
            P("expert", "tensor", "section"),
            P("expert", "tensor", "section"),
            P("expert", "tensor", None),
            P("expert", "tensor", None),
            P("expert", None, "tensor"),
            P("expert", None, "tensor"),
            P("expert", "tensor", None),
        ),
        out_specs=P("expert", "tensor", "section"),
        check_vma=False,
    )
```

time: 315 us -> 135 us (0.43)
  the two profiles are of different devices: /device:TPU:96 before, /device:TPU:1 now
where the time goes in v3:
time: 135 us
  Pallas kernels  134 us (99%)
  local copies, waits for them, and re-layouts  1.67 us (1%)
    pallas_call x1, Pallas kernels, on_device(): pl.pallas_call(layer_kernel, out_shape=jax.ShapeDtypeStruct(query.shape,...  134 us

profile of v3, /device:TPU:1, one launch (start us, length us, event | category | flops | bytes accessed | tf_op | source)
XLA Modules:
  0.0 135.2 jit_solution(11603400938404017588)
XLA Ops:
  0.0 133.5 %layer.1 = bf16[1,64,2048]{2,1,0:T(8,128)(2,1)} custom-call(bf16[1,64,2048]{2,1,0:T(8,128)(2,1)} %q_any.1, bf16[1,64,512]{2,1,0:T(8,128)(2,1)} %k_any.1, bf16[1,64,512]{2,1,0:T(8,128)(2,1)} %v_any.1, bf16[1,64,2048]{2,1,0:T(8,128)(2,1)} %res_any.1, s32[2,64]{1,0:T(2,128)} %bitcast.6, f32[2,64]{1,0:T(2,128)} %bitcast.7, bf16[1,4096,512]{2,1,0:T(8,128)(2,1)} %wg_any.1, ...), custom_call_target="tpu_custom_call" | custom-call | tf_op jit(solution)/shard_map/layer/pallas_call | solution.py:746
  133.6 1.7 %copy.11 = bf16[1,64,2048]{2,1,0:T(8,128)(2,1)} copy(bf16[1,64,2048]{2,1,0:T(8,128)(2,1)} %layer.1) | data formatting | bytes 524288

commit v4 on v3

--- a/solution.py
+++ b/solution.py
@@ -24,6 +24,10 @@
 
 def dot(a, b):
     return jnp.dot(a, b, preferred_element_type=F32)
+
+
+def landed(ref, sem):
+    pltpu.make_async_copy(ref, ref, sem).wait()
 
 
 def dot_rows(a, b):
@@ -53,10 +57,10 @@
     own_in = []
     for h in range(kv_heads):
         at = pl.ds(HD * h, HD)
-        own_in.append(pltpu.make_async_copy(k_any.at[0, :, at], kv.at[7, 0, h, 0], in_sem.at[2 * h]))
-        own_in.append(pltpu.make_async_copy(v_any.at[0, :, at], kv.at[7, 0, h, 1], in_sem.at[2 * h + 1]))
-    queries_in = pltpu.make_async_copy(q_any.at[0], qv, in_sem.at[8])
-    residual_in = pltpu.make_async_copy(res_any.at[0], res, in_sem.at[9])
+        own_in.append(pltpu.make_async_copy(k_any.at[0, :, at], kv.at[7, 0, h, 0], in_sem.at[0]))
+        own_in.append(pltpu.make_async_copy(v_any.at[0, :, at], kv.at[7, 0, h, 1], in_sem.at[0]))
+    queries_in = pltpu.make_async_copy(q_any.at[0], qv, in_sem.at[1])
+    residual_in = pltpu.make_async_copy(res_any.at[0], res, in_sem.at[2])
     own_in += [queries_in, residual_in]
     for load in own_in:
         load.start()
@@ -89,18 +93,17 @@
     def spread(way, d, h):
         return copy_to(
             kv.at[slot(way, d), 0, h], kv.at[slot(way, d + 1), 0, h],
-            kg_s.at[way, 4 * d + h], kg_r.at[way, 4 * d + h], ring[way],
+            kg_s.at[way, d // 3], kg_r.at[way, 4 * d + h], ring[way],
         )
 
     def swap(k, h):
-        return copy_to(kv.at[k, 0, h], kv.at[k, 1, h], kx_s.at[k, h], kx_r.at[k, h], partner)
+        return copy_to(kv.at[k, 0, h], kv.at[k, 1, h], kx_s.at[0], kx_r.at[k, h], partner)
 
     tell = [
-        copy_to(rz.at[7], rz.at[FAR[k - 1]], rz_s.at[k - 1], rz_r.at[k - 1], (s, e, ((z + k) % NZ) * 2 + c))
+        copy_to(rz.at[7], rz.at[FAR[k - 1]], rz_s.at[0], rz_r.at[0], (s, e, ((z + k) % NZ) * 2 + c))
         for k in range(1, NZ)
     ]
-    for load in own_in[:8]:
-        load.wait()
+    landed(kv.at[7, 0], in_sem.at[0])
     pl.semaphore_wait(barrier, 38)
     for h in range(kv_heads):
         for way in range(2):
@@ -201,8 +204,7 @@
         return carry
 
     bias4 = ring_bias(4)
-    for copy in tell:
-        copy.wait_recv()
+    landed(rz.at[pl.ds(0, 7)], rz_r.at[0])
     for k in range(7):
         slot_tables(k)
     for h in range(2):
@@ -217,7 +219,6 @@
     rings = (half - wide) // RING
     ring_half = (tuple(range((rings + 1) // 2)), tuple(range((rings + 1) // 2, rings)))
     hw = half // kv_heads
-    sent, own_sent = [], []
 
     def ring_cols(j):
         return pl.ds(wide + RING * j, RING)
@@ -225,16 +226,21 @@
     def send(copy, i, same):
         if i == 0 and same:
             pl.when(jnp.logical_not(own))(copy.start)
-            own_sent.append(copy)
         else:
             copy.start()
-            sent.append(copy)
-
-    def receive(copy, i, same):
-        if i == 0 and same:
-            pl.when(jnp.logical_not(own))(copy.wait_recv)
-        else:
-            copy.wait_recv()
+
+    def settle(ref, sem, axis):
+        index = [slice(None)] * len(ref.shape)
+        index[axis] = pl.ds(0, ref.shape[axis] - ref.shape[axis] // (16 if ref.shape[axis] > 8 else 8))
+        fewer = tuple(pl.ds(0, n) if isinstance(i, slice) else i for i, n in zip(index, ref.shape))
+
+        @pl.when(own)
+        def _():
+            landed(ref.at[fewer], sem)
+
+        @pl.when(jnp.logical_not(own))
+        def _():
+            landed(ref, sem)
 
     def source_rows(ef, cf):
         return pl.ds(pl.multiple_of((ef * 2 + cf) * SLOTS, SLOTS), SLOTS)
@@ -246,7 +252,7 @@
                 at = pl.ds(wide // 2 * j, wide // 2)
                 carry_on[way, d, j] = copy_to(
                     hz.at[slot(way, d), :, at], hz.at[slot(way, d + 1), :, at],
-                    hz_s.at[way, 2 * d + j], hz_r.at[way, 2 * d + j], ring[way],
+                    hz_s.at[way, d // 3], hz_r.at[way, 2 * d + j], ring[way],
                 )
 
     for h in range(kv_heads):
@@ -291,10 +297,10 @@
                 send(
                     copy_to(
                         pk.at[ed * 2 + sd, :, part], xm.at[7, source_rows(e, c), land],
-                        d_s.at[a, i * 2 + k], d_r.at[a, e * 2 + c], (sd, ed, z * 2 + s),
+                        d_s.at[a], d_r.at[a], (sd, ed, z * 2 + s),
                     ), i, k == 0,
                 )
-            send(copy_to(pov.at[a, ed], ovr.at[a, e], o_s.at[a, i], o_r.at[a, e], (c, ed, z * 2 + s)), i, True)
+            send(copy_to(pov.at[a, ed], ovr.at[a, e], o_s.at[a], o_r.at[a], (c, ed, z * 2 + s)), i, True)
 
     groups = ((7, 1), (0, 2), (2, 2), (4, 2), (6, 1))
 
@@ -322,11 +328,11 @@
                 send(
                     copy_to(
                         pw.at[w, ed * 2 + sd, many], xm.at[slots, source_rows(e, c), at],
-                        dw_s.at[w, i * 2 + k], dw_r.at[w, e * 2 + c], (sd, ed, z * 2 + s),
+                        dw_s.at[w], dw_r.at[w], (sd, ed, z * 2 + s),
                     ), i, k == 0,
                 )
             send(
-                copy_to(pvw.at[w, ed, many], ovw.at[w, e, many], ow_s.at[w, i], ow_r.at[w, e], (c, ed, z * 2 + s)),
+                copy_to(pvw.at[w, ed, many], ovw.at[w, e, many], ow_s.at[w], ow_r.at[w], (c, ed, z * 2 + s)),
                 i, True,
             )
 
@@ -335,20 +341,8 @@
         many = pl.ds(0, count)
         slots = pl.ds(start, count)
         at = pl.ds(0, wide)
-        for i in range(8):
-            ef = (e + 8 - i) % 8
-            for k in range(2):
-                cf = (c + k) % 2
-                receive(
-                    copy_to(
-                        pw.at[w, 0, many], xm.at[slots, source_rows(ef, cf), at],
-                        dw_s.at[w, 0], dw_r.at[w, ef * 2 + cf], (c, ef, z * 2 + cf),
-                    ), i, k == 0,
-                )
-            receive(
-                copy_to(pvw.at[w, 0, many], ovw.at[w, ef, many], ow_s.at[w, 0], ow_r.at[w, ef], (c, ef, z * 2 + s)),
-                i, True,
-            )
+        settle(xm.at[slots, pl.ds(0, MAIN), at], dw_r.at[w], 1)
+        settle(ovw.at[w, :, many], ow_r.at[w], 0)
         for p in range(count):
             for q in range(wide // 128):
                 xm[start + p, MAIN:, 128 * q : 128 * (q + 1)] = ovw[w, :, p, q, :].astype(BF)
@@ -374,17 +368,17 @@
                 n = d * rings + j
                 gather[way, d, j] = copy_to(
                     xm.at[slot(way, d), :, ring_cols(j)], xm.at[slot(way, d + 1), :, ring_cols(j)],
-                    ag_s.at[way, n], ag_r.at[way, n], ring[way],
+                    ag_s.at[way, d // 3], ag_r.at[way, n], ring[way],
                 )
     for k in range(8):
         for n, (begin, end) in enumerate(parts):
             at = pl.ds(begin, end - begin)
-            share[k, n] = copy_to(xm.at[k, :, at], xp.at[k, :, at], xs.at[k, n], xrs.at[k, n], partner)
+            share[k, n] = copy_to(xm.at[k, :, at], xp.at[k, :, at], xs.at[0], xrs.at[k, n], partner)
 
     def trade(g, j):
         at = pl.ds(pl.multiple_of(j * cw, cw), cw)
         pair = pl.ds(2 * g - 2, 2)
-        return copy_to(yps.at[pair, :, at], ypr.at[pair, :, at], yss.at[g - 1, j], yrs.at[g - 1, j], partner)
+        return copy_to(yps.at[pair, :, at], ypr.at[pair, :, at], yss.at[0], yrs.at[g - 1, j], partner)
 
     def hidden_units(g, first, last):
         def piece(k, carry):
@@ -449,13 +443,13 @@
                 n = (d - 1) * rings + j
                 reduce[way, d, j] = copy_to(
                     ys.at[target, :, ring_cols(j)], rr.at[way, d - 1, :, pl.ds(RING * j, RING)],
-                    rs_s.at[way, n], rs_r.at[way, n], ring[way],
+                    rs_s.at[way, d // 4], rs_r.at[way, n], ring[way],
                 )
             for j in range(2) if d < 4 else (way,):
                 at = pl.ds(wide // 2 * j, wide // 2)
                 link[way, d, j] = copy_to(
                     cz.at[target, :, at], rc.at[way, d - 1, :, at],
-                    cr_s.at[way, 2 * (d - 1) + j], cr_r.at[way, 2 * (d - 1) + j], ring[way],
+                    cr_s.at[way, d // 4], cr_r.at[way, 2 * (d - 1) + j], ring[way],
                 )
 
     def pass_on(way, d, j, add):
@@ -508,31 +502,19 @@
                 send(
                     copy_to(
                         ys.at[slots, source_rows(ed, cd), at], rb.at[w, e * 2 + s, many],
-                        bw_s.at[w, i * 2 + k], bw_r.at[w, e * 2 + s], (c, ed, z * 2 + cd),
+                        bw_s.at[w], bw_r.at[w], (c, ed, z * 2 + cd),
                     ), i, k == 0,
                 )
             send(
-                copy_to(pvb.at[w, ed, many], ovb.at[w, e, many], vw_s.at[w, i], vw_r.at[w, e], (c, ed, z * 2 + s)),
+                copy_to(pvb.at[w, ed, many], ovb.at[w, e, many], vw_s.at[w], vw_r.at[w], (c, ed, z * 2 + s)),
                 i, True,
             )
 
     def receive_back(w):
         start, count = groups[w]
         many, slots, at = pl.ds(0, count), pl.ds(start, count), pl.ds(0, wide)
-        for i in range(8):
-            ef = (e + 8 - i) % 8
-            for k in range(2):
-                sf = (s + k) % 2
-                receive(
-                    copy_to(
-                        ys.at[slots, source_rows(0, 0), at], rb.at[w, ef * 2 + sf, many],
-                        bw_s.at[w, 0], bw_r.at[w, ef * 2 + sf], (sf, ef, z * 2 + s),
-                    ), i, k == 0,
-                )
-            receive(
-                copy_to(pvb.at[w, 0, many], ovb.at[w, ef, many], vw_s.at[w, 0], vw_r.at[w, ef], (c, ef, z * 2 + s)),
-                i, True,
-            )
+        settle(rb.at[w, :, many], bw_r.at[w], 0)
+        settle(ovb.at[w, :, many], vw_r.at[w], 0)
         totals = []
         for p in range(count):
             extra = jnp.concatenate([ovb[w, :, p, q, :] for q in range(wide // 128)], axis=1).astype(BF)
@@ -549,17 +531,8 @@
         width = hw * (a + 2) - from_col
         land = pl.ds(from_col, width)
         part = pl.ds(from_col - wide, width)
-        for i in range(8):
-            ef = (e + 8 - i) % 8
-            for k in range(2):
-                cf = (c + k) % 2
-                receive(
-                    copy_to(
-                        pk.at[0, :, part], xm.at[7, source_rows(ef, cf), land],
-                        d_s.at[a, 0], d_r.at[a, ef * 2 + cf], (c, ef, z * 2 + cf),
-                    ), i, k == 0,
-                )
-            receive(copy_to(pov.at[a, 0], ovr.at[a, ef], o_s.at[a, 0], o_r.at[a, ef], (c, ef, z * 2 + s)), i, True)
+        settle(xm.at[7, pl.ds(0, MAIN), land], d_r.at[a], 0)
+        settle(ovr.at[a], o_r.at[a], 0)
         for q in range(width // 128):
             at = from_col + 128 * q
             xm[7, MAIN:, at : at + 128] = ovr[a, :, q, :].astype(BF)
@@ -682,10 +655,10 @@
                 send(
                     copy_to(
                         ys.at[7, source_rows(ed, cd), land], ret.at[e * 2 + s, :, part],
-                        b_s.at[a, i * 2 + k], b_r.at[a, e * 2 + s], (c, ed, z * 2 + cd),
+                        b_s.at[a], b_r.at[a], (c, ed, z * 2 + cd),
                     ), i, k == 0,
                 )
-            send(copy_to(fov.at[a, ed], retov.at[a, e], bo_s.at[a, i], bo_r.at[a, e], (c, ed, z * 2 + s)), i, True)
+            send(copy_to(fov.at[a, ed], retov.at[a, e], bo_s.at[a], bo_r.at[a], (c, ed, z * 2 + s)), i, True)
 
     total = receive_back(0)
     for way in range(2):
@@ -697,42 +670,42 @@
     for a, (j, count) in enumerate(pieces):
         width = count * RING
         land, part = pl.ds(wide + RING * j, width), pl.ds(RING * j, width)
-        for i in range(8):
-            ef = (e + 8 - i) % 8
-            for k in range(2):
-                sf = (s + k) % 2
-                receive(
-                    copy_to(
-                        ys.at[7, source_rows(0, 0), land], ret.at[ef * 2 + sf, :, part],
-                        b_s.at[a, 0], b_r.at[a, ef * 2 + sf], (sf, ef, z * 2 + s),
-                    ), i, k == 0,
-                )
-            receive(copy_to(fov.at[a, 0], retov.at[a, ef], bo_s.at[a, 0], bo_r.at[a, ef], (c, ef, z * 2 + s)), i, True)
+        settle(ret.at[:, :, part], b_r.at[a], 0)
+        settle(retov.at[a], bo_r.at[a], 0)
         extra = jnp.concatenate([retov[a, :, q, :] for q in range(width // 128)], axis=1).astype(BF)
         total = weigh(7, ret[:, :, part].reshape(MAIN, width), extra)
         out[0, :, land] = (hid[:, land].astype(F32) + total).astype(BF)
 
-    @pl.when(jnp.logical_not(own))
-    def _():
-        for copy in own_sent:
-            copy.wait_send()
-    for copy in sent:
-        copy.wait_send()
+    for a in range(3):
+        from_col = max(wide, hw * (a + 1))
+        part = pl.ds(from_col - wide, hw * (a + 2) - from_col)
+        settle(pk.at[:, :, part], d_s.at[a], 0)
+        settle(pov.at[a], o_s.at[a], 0)
+        settle(ret.at[:, :, pl.ds(RING * pieces[a][0], RING * pieces[a][1])], b_s.at[a], 0)
+        settle(fov.at[a], bo_s.at[a], 0)
+    for w, (start, count) in enumerate(groups):
+        many = pl.ds(0, count)
+        settle(pw.at[w, :, many], dw_s.at[w], 0)
+        settle(pvw.at[w, :, many], ow_s.at[w], 0)
+        settle(rb.at[w, :, many], bw_s.at[w], 0)
+        settle(pvb.at[w, :, many], vw_s.at[w], 0)
+    some = pl.ds(0, 3)
+    rest = pl.ds(0, wide // 2)
     for way in range(2):
-        for d in range(4):
-            for h in range(kv_heads) if d < 3 else half_of[way]:
-                spread(way, d, h).wait_send()
-    for k in range(8):
-        for h in range(kv_heads):
-            swap(k, h).wait_send()
-    for copy in tell:
-        copy.wait_send()
-    for g in range(1, 5):
-        for j in range(CHUNKS):
-            trade(g, j).wait_send()
-    for table in (carry_on, gather, share, reduce, link):
-        for copy in table.values():
-            copy.wait_send()
+        landed(kv.at[some, 0], kg_s.at[way, 0])
+        landed(kv.at[0, 0, pl.ds(0, 2)], kg_s.at[way, 1])
+        landed(hz.at[some], hz_s.at[way, 0])
+        landed(hz.at[0, :, rest], hz_s.at[way, 1])
+        landed(xm.at[some, :, pl.ds(wide, half - wide)], ag_s.at[way, 0])
+        landed(xm.at[0, :, pl.ds(wide, RING * len(ring_half[way]))], ag_s.at[way, 1])
+        landed(ys.at[some, :, pl.ds(wide, half - wide)], rs_s.at[way, 0])
+        landed(ys.at[0, :, pl.ds(wide, RING * len(ring_half[way]))], rs_s.at[way, 1])
+        landed(cz.at[some], cr_s.at[way, 0])
+        landed(cz.at[0, :, rest], cr_s.at[way, 1])
+    landed(kv.at[:, 0], kx_s.at[0])
+    landed(rz.at[pl.ds(0, 7)], rz_s.at[0])
+    landed(xm, xs.at[0])
+    landed(yps, yss.at[0])
 
 
 def on_device(query, keys, values, residual, routes, gates, w_gate, w_up, w_down):
@@ -790,12 +763,12 @@
             pltpu.VMEM((5, 8, 2, 8, 128), F32),
             pltpu.VMEM((8, tokens, WIDE), BF),
             pltpu.VMEM((2, 4, tokens, WIDE), BF),
-            dma((10,)), dma((7,)), dma((7,)), dma((2, 16)), dma((2, 16)), dma((8, 4)), dma((8, 4)),
-            dma((2, 8)), dma((2, 8)), dma((5, 16)), dma((5, 16)), dma((5, 8)), dma((5, 8)),
-            dma((6,)), dma((3, 16)), dma((3, 16)), dma((3, 8)), dma((3, 8)),
-            dma((2, 32)), dma((2, 32)), dma((8, 3)), dma((8, 3)), dma((4, 4)), dma((4, 4)),
-            dma((2, 32)), dma((2, 32)), dma((3, 16)), dma((3, 16)), dma((3, 8)), dma((3, 8)),
-            dma((5, 16)), dma((5, 16)), dma((5, 8)), dma((5, 8)), dma((2, 8)), dma((2, 8)),
+            dma((3,)), dma((1,)), dma((1,)), dma((2, 2)), dma((2, 16)), dma((1,)), dma((8, 4)),
+            dma((2, 2)), dma((2, 8)), dma((5,)), dma((5,)), dma((5,)), dma((5,)),
+            dma((6,)), dma((3,)), dma((3,)), dma((3,)), dma((3,)),
+            dma((2, 2)), dma((2, 20)), dma((1,)), dma((8, 3)), dma((1,)), dma((4, 4)),
+            dma((2, 2)), dma((2, 20)), dma((3,)), dma((3,)), dma((3,)), dma((3,)),
+            dma((5,)), dma((5,)), dma((5,)), dma((5,)), dma((2, 2)), dma((2, 8)),
         ],
         compiler_params=pltpu.CompilerParams(
             collective_id=1, has_side_effects=True, vmem_limit_bytes=60 * 1024 * 1024

time: 135 us -> 125 us (0.926)
  Pallas kernels: 134 us -> 123 us
    pallas_call x1, Pallas kernels: 134 us -> 123 us  [on_device(): pl.pallas_call(layer_kernel, out_shape=jax.ShapeDtypeStruct(query.shape,...]
where the time goes in v4:
time: 125 us
  Pallas kernels  123 us (98%)
  local copies, waits for them, and re-layouts  1.67 us (1%)
    pallas_call x1, Pallas kernels, on_device(): pl.pallas_call(layer_kernel, out_shape=jax.ShapeDtypeStruct(query.shape,...  123 us

profile of v4, /device:TPU:1, one launch (start us, length us, event | category | flops | bytes accessed | tf_op | source)
XLA Modules:
  0.0 125.2 jit_solution(1834173354838667259)
XLA Ops:
  0.0 123.5 %layer.1 = bf16[1,64,2048]{2,1,0:T(8,128)(2,1)} custom-call(bf16[1,64,2048]{2,1,0:T(8,128)(2,1)} %q_any.1, bf16[1,64,512]{2,1,0:T(8,128)(2,1)} %k_any.1, bf16[1,64,512]{2,1,0:T(8,128)(2,1)} %v_any.1, bf16[1,64,2048]{2,1,0:T(8,128)(2,1)} %res_any.1, s32[2,64]{1,0:T(2,128)} %bitcast.6, f32[2,64]{1,0:T(2,128)} %bitcast.7, bf16[1,4096,512]{2,1,0:T(8,128)(2,1)} %wg_any.1, ...), custom_call_target="tpu_custom_call" | custom-call | tf_op jit(solution)/shard_map/layer/pallas_call | solution.py:719
  123.5 1.7 %copy.11 = bf16[1,64,2048]{2,1,0:T(8,128)(2,1)} copy(bf16[1,64,2048]{2,1,0:T(8,128)(2,1)} %layer.1) | data formatting | bytes 524288

commit v5 on v4

--- a/solution.py
+++ b/solution.py
@@ -586,7 +586,6 @@
         share[slot(way, 3), 0].wait_recv()
     units_part(3, 0, False, True)
     down_out(3)
-    down_out(2)
     for way in range(2):
         for j in ring_half[way]:
             gather[way, 3, j].wait_recv()
@@ -599,13 +598,13 @@
     lasts = (orders[0], (0, 3, 4, 1, 2))
     both_ways(3, swapped, False)
     send_back(3)
-    down_own(2)
+    down_out(2)
     shared(6)
     shared(7)
-    hidden_units(4, 0, 1)
+    hidden_units(4, 0, 2)
+    down_out(4)
+    down_own(2)
     both_ways(2, swapped, True)
-    hidden_units(4, 1, 2)
-    down_out(4)
     down_own(4)
     both_ways(4, ring_half, False)
     send_back(4)
@@ -625,8 +624,8 @@
     chain(2)
     receive_back(1)
     both_ways(1, tuple(o[2:4] for o in lasts), True)
+    both_ways(1, tuple(o[4:] for o in lasts), True)
     chain(1)
-    both_ways(1, tuple(o[4:] for o in lasts), True)
 
     pieces = ((3, 2), (0, 2), (2, 1))
     for a, (j, count) in enumerate(pieces):

time: 125 us -> 121 us (0.968)
  Pallas kernels: 123 us -> 119 us
    pallas_call x1, Pallas kernels: 123 us -> 119 us  [on_device(): pl.pallas_call(layer_kernel, out_shape=jax.ShapeDtypeStruct(query.shape,...]
where the time goes in v5:
time: 121 us
  Pallas kernels  119 us (98%)
  local copies, waits for them, and re-layouts  1.67 us (1%)
    pallas_call x1, Pallas kernels, on_device(): pl.pallas_call(layer_kernel, out_shape=jax.ShapeDtypeStruct(query.shape,...  119 us

profile of v5, /device:TPU:1, one launch (start us, length us, event | category | flops | bytes accessed | tf_op | source)
XLA Modules:
  0.0 121.1 jit_solution(15492151747139378897)
XLA Ops:
  0.0 119.5 %layer.1 = bf16[1,64,2048]{2,1,0:T(8,128)(2,1)} custom-call(bf16[1,64,2048]{2,1,0:T(8,128)(2,1)} %q_any.1, bf16[1,64,512]{2,1,0:T(8,128)(2,1)} %k_any.1, bf16[1,64,512]{2,1,0:T(8,128)(2,1)} %v_any.1, bf16[1,64,2048]{2,1,0:T(8,128)(2,1)} %res_any.1, s32[2,64]{1,0:T(2,128)} %bitcast.6, f32[2,64]{1,0:T(2,128)} %bitcast.7, bf16[1,4096,512]{2,1,0:T(8,128)(2,1)} %wg_any.1, ...), custom_call_target="tpu_custom_call" | custom-call | tf_op jit(solution)/shard_map/layer/pallas_call | solution.py:718
  119.5 1.7 %copy.11 = bf16[1,64,2048]{2,1,0:T(8,128)(2,1)} copy(bf16[1,64,2048]{2,1,0:T(8,128)(2,1)} %layer.1) | data formatting | bytes 524288

commit v6 on v5

--- a/solution.py
+++ b/solution.py
@@ -578,7 +578,6 @@
                 for way in range(2):
                     share[slot(way, 3), 1].wait_recv()
                 units_part(3, 1, True, False)
-    receive_wide(4)
     for way in range(2):
         share[slot(way, 3), 2].wait_recv()
     units_part(3, 2, False, False)
@@ -586,6 +585,7 @@
         share[slot(way, 3), 0].wait_recv()
     units_part(3, 0, False, True)
     down_out(3)
+    receive_wide(4)
     for way in range(2):
         for j in ring_half[way]:
             gather[way, 3, j].wait_recv()
@@ -621,9 +621,9 @@
     chain(3)
     receive_back(2)
     both_ways(1, tuple(o[:2] for o in lasts), True)
+    both_ways(1, tuple(o[2:4] for o in lasts), True)
     chain(2)
     receive_back(1)
-    both_ways(1, tuple(o[2:4] for o in lasts), True)
     both_ways(1, tuple(o[4:] for o in lasts), True)
     chain(1)
 

time: 121 us -> 122 us (level)
  no operation moved by 1% of the time
where the time goes in v6:
time: 122 us
  Pallas kernels  120 us (98%)
  local copies, waits for them, and re-layouts  1.67 us (1%)
    pallas_call x1, Pallas kernels, on_device(): pl.pallas_call(layer_kernel, out_shape=jax.ShapeDtypeStruct(query.shape,...  120 us

profile of v6, /device:TPU:1, one launch (start us, length us, event | category | flops | bytes accessed | tf_op | source)
XLA Modules:
  0.0 122.0 jit_solution(12900750642092698274)
XLA Ops:
  0.0 120.4 %layer.1 = bf16[1,64,2048]{2,1,0:T(8,128)(2,1)} custom-call(bf16[1,64,2048]{2,1,0:T(8,128)(2,1)} %q_any.1, bf16[1,64,512]{2,1,0:T(8,128)(2,1)} %k_any.1, bf16[1,64,512]{2,1,0:T(8,128)(2,1)} %v_any.1, bf16[1,64,2048]{2,1,0:T(8,128)(2,1)} %res_any.1, s32[2,64]{1,0:T(2,128)} %bitcast.6, f32[2,64]{1,0:T(2,128)} %bitcast.7, bf16[1,4096,512]{2,1,0:T(8,128)(2,1)} %wg_any.1, ...), custom_call_target="tpu_custom_call" | custom-call | tf_op jit(solution)/shard_map/layer/pallas_call | solution.py:718
  120.4 1.7 %copy.11 = bf16[1,64,2048]{2,1,0:T(8,128)(2,1)} copy(bf16[1,64,2048]{2,1,0:T(8,128)(2,1)} %layer.1) | data formatting | bytes 524288
